TPU v7x, 128 devices: a whole 4x4x4 slice. The times are simulated.
128 devices in a mesh: data: 1, row: 2 (over core), col: 64 (over z, y, x).
Axes of the slice: x: 4, y: 4, z: 4, core: 2. Of those that a mesh axis runs over, the one named last changes fastest.
Arguments:
- tokens: bfloat16 [16384, 2048], P(('data', 'row', 'col'))
- expert_ids: int32 [16384, 8], P(('data', 'row', 'col'))
- gate_weights: float32 [16384, 8], P(('data', 'row', 'col'))
- w_in: bfloat16 [128, 2048, 768], P(('row', 'col'))
- w_out: bfloat16 [128, 768, 2048], P(('row', 'col'))
Outputs:
- output: bfloat16 [16384, 2048], P(('data', 'row', 'col'))
All inputs are finite; a program needn't handle non-finite values.
Results may differ from a plain program's by a relative error of at most 0.00451473.
Values are sent between devices in bfloat16 or wider.
A program may use at most 1 GiB of HBM per device.

v0:
```python
import jax
import jax.numpy as jnp
from jax import lax
from jax.sharding import PartitionSpec as P

GRID_AXES = ('row', 'col')


def local_ranks(flat_ids, num_experts):
    pair_count = flat_ids.shape[0]
    sort_order = jnp.argsort(flat_ids, stable=True)
    counts = jnp.zeros((num_experts,), jnp.int32).at[flat_ids].add(1)
    starts = jnp.cumsum(counts) - counts
    sorted_rank = jnp.arange(pair_count, dtype=jnp.int32) - starts[flat_ids[sort_order]]
    pair_rank = jnp.zeros((pair_count,), jnp.int32).at[sort_order].set(sorted_rank)
    return counts, pair_rank


def solution(mesh):
    rows_n = mesh.shape['row']
    cols_n = mesh.shape['col']
    group_size = rows_n * cols_n

    def device_fn(tokens, expert_ids, gate_weights, w_in, w_out):
        tok_dev, model_width = tokens.shape
        top_k = expert_ids.shape[1]
        local_experts = w_in.shape[0]
        num_experts = local_experts * group_size
        capacity = tok_dev * group_size * top_k // num_experts
        per_source = 2 * tok_dev * top_k // num_experts
        flat_ids = expert_ids.reshape(-1)
        pair_count = flat_ids.shape[0]
        counts, pair_rank = local_ranks(flat_ids, num_experts)

        col_counts = lax.all_gather(counts, 'col')
        col_before = jnp.arange(cols_n)[:, None] < lax.axis_index('col')
        before_col = jnp.sum(jnp.where(col_before, col_counts, 0), axis=0)
        row_totals = lax.all_gather(jnp.sum(col_counts, axis=0), 'row')
        row_before = jnp.arange(rows_n)[:, None] < lax.axis_index('row')
        before_row = jnp.sum(jnp.where(row_before, row_totals, 0), axis=0)
        offsets = before_row + before_col

        global_rank = offsets[flat_ids] + pair_rank
        send_pos = flat_ids * per_source + pair_rank
        send_token = jnp.where(global_rank < capacity, jnp.arange(pair_count, dtype=jnp.int32) // top_k, tok_dev)
        send_index = jnp.full((num_experts * per_source,), tok_dev, jnp.int32).at[send_pos].set(send_token)
        send_rows = jnp.take(tokens, send_index, axis=0, mode='fill', fill_value=0)
        send_rows = send_rows.reshape(group_size, local_experts, per_source, model_width)
        meta_send = jnp.stack([offsets, counts], axis=-1).reshape(group_size, local_experts, 2)

        meta_recv = lax.all_to_all(meta_send, GRID_AXES, 0, 0, tiled=True)
        recv_rows = lax.all_to_all(send_rows, GRID_AXES, 0, 0, tiled=True)

        source_off = meta_recv[:, :, 0]
        source_cnt = meta_recv[:, :, 1]
        source_end = source_off + source_cnt
        slot_pos = jnp.arange(capacity)
        slot_source = jnp.sum(source_end.T[:, None, :] <= slot_pos[None, :, None], axis=-1)
        source_clip = jnp.minimum(slot_source, group_size - 1)
        slot_start = jnp.take_along_axis(source_off.T, source_clip, axis=1)
        expert_pos = jnp.arange(local_experts)[:, None]
        recv_index = (source_clip * local_experts + expert_pos) * per_source + slot_pos[None, :] - slot_start
        recv_index = jnp.where(slot_source < group_size, recv_index, group_size * local_experts * per_source)
        buffer = jnp.take(recv_rows.reshape(-1, model_width), recv_index.reshape(-1), axis=0, mode='fill', fill_value=0)
        buffer = buffer.reshape(local_experts, capacity, model_width)

        hidden = jax.nn.gelu(jnp.einsum('ecd,edf->ecf', buffer, w_in, preferred_element_type=jnp.float32)).astype(jnp.bfloat16)
        expert_out = jnp.einsum('ecf,efd->ecd', hidden, w_out, preferred_element_type=jnp.float32).astype(jnp.bfloat16)

        back_pos = jnp.arange(per_source)
        back_slot = source_off[:, :, None] + back_pos
        back_valid = (back_pos < source_cnt[:, :, None]) & (back_slot < capacity)
        back_index = jnp.where(back_valid, jnp.arange(local_experts)[None, :, None] * capacity + back_slot, local_experts * capacity)
        back_rows = jnp.take(expert_out.reshape(-1, model_width), back_index.reshape(-1), axis=0, mode='fill', fill_value=0)
        back_rows = back_rows.reshape(group_size, local_experts, per_source, model_width)
        returned = lax.all_to_all(back_rows, GRID_AXES, 0, 0, tiled=True)

        pair_rows = jnp.take(returned.reshape(-1, model_width), send_pos, axis=0, mode='fill', fill_value=0).reshape(tok_dev, top_k, model_width)
        mixed_sum = jnp.einsum('tk,tkd->td', gate_weights, pair_rows, preferred_element_type=jnp.float32)
        return (tokens.astype(jnp.float32) + mixed_sum).astype(jnp.bfloat16)

    token_spec = P(('data', 'row', 'col'), None)
    expert_spec = P(GRID_AXES, None, None)
    return jax.shard_map(device_fn, mesh=mesh, in_specs=(token_spec, token_spec, token_spec, expert_spec, expert_spec), out_specs=token_spec, check_vma=False)
```

profile of v0, /device:TPU:1, one launch (start us, length us, event | category | flops | bytes accessed | tf_op | source)
XLA Modules:
  0.0 601.6 jit_solution(15321848833365038190)
XLA Ops:
  0.0 0.0 copy-start
  0.0 0.9 copy.22
  0.9 0.1 reshape.379
  1.1 7.6 %scatter_custom_fusion = s32[128]{0:T(128)S(1)} fusion(s32[1024]{0:T(1024)S(1)} %bitcast.54, s32[1024]{0:T(1024)S(1)} %broadcast.289, s32[]{:T(128)} %constant.54.clone.1), kind=kCustom, calls=%fused_computation.95 | custom fusion | flops 1024 | bytes 516 | tf_op jit(solution)/shard_map/scatter-add | solution.py:12
  8.7 151.0 %all-gather.2 = s32[64,1,128]{2,1,0:T(1,128)S(1)} all-gather(s32[1,1,128]{2,1,0:T(1,128)S(1)} %bitcast.60), channel_id=2, replica_groups=mesh['data'=1,'row'=2,'col'=64] {'col'}, dimensions={0}, use_global_device_ids=true | all-gather | bytes 33280 | tf_op jit(solution)/shard_map/all_gather | solution.py:35
  159.7 0.1 reduce_sum.36
  159.8 30.2 %all-gather.3 = s32[2,1,128]{2,1,0:T(1,128)S(1)} all-gather(s32[1,1,128]{2,1,0:T(1,128)S(1)} %bitcast.65), channel_id=3, replica_groups=mesh['data'=1,'row'=2,'col'=64] {'row'}, dimensions={0}, use_global_device_ids=true | all-gather | bytes 1536 | tf_op jit(solution)/shard_map/all_gather | solution.py:38
  190.0 0.1 select_reduce_fusion.1
  190.1 0.1 select_reduce_fusion
  190.2 0.7 copy.25
  190.9 3.7 all-to-all-start
  194.7 0.1 copy.24
  194.8 0.1 reshape.381
  194.9 0.2 reduce-window.9
  195.1 0.1 reduce.2
  195.2 4.4 sort.17
  199.6 4.5 gather_fusion
  204.1 6.6 %gather_fusion.1 = s32[1024]{0:T(1024)S(1)} fusion(s32[128]{0:T(128)S(1)} %sub.18, s32[1024]{0:T(1024)S(1)} %broadcast_clamp_fusion.5), kind=kCustom, calls=%fused_computation.3 | custom fusion | bytes 12288 | tf_op jit(solution)/shard_map/gather | solution.py:14
  210.7 6.6 %gather_fusion.2 = s32[1024]{0:T(1024)S(1)} fusion(s32[128]{0:T(128)S(1)} %add.171, s32[1024]{0:T(1024)S(1)} %broadcast_clamp_fusion.3), kind=kCustom, calls=%fused_computation.4 | custom fusion | bytes 12288 | tf_op jit(solution)/shard_map/gather | solution.py:43
  217.3 4.3 scatter_custom_fusion.1
  221.6 4.3 scatter_custom_fusion.2
  226.0 0.1 broadcast_in_dim.102
  226.1 17.4 %gather_fusion.3 = bf16[2048,2048]{1,0:T(8,128)(2,1)} fusion(bf16[128,2048]{1,0:T(8,128)(2,1)} %param.7, s32[2048]{0:T(1024)S(1)} %fusion.38), kind=kCustom, calls=%fused_computation.5 | custom fusion | bytes 16785408 | tf_op jit(solution)/shard_map/jit(_take)/gather | solution.py:47
  243.5 7.3 %broadcast_select_fusion = bf16[128,1,16,2048]{3,2,1,0:T(8,128)(2,1)} fusion(bf16[128,1,16,2048]{3,2,1,0:T(8,128)(2,1)} %bitcast.51, pred[128,16]{1,0:T(8,128)(4,1)S(1)} %broadcast_in_dim.102), kind=kLoop, calls=%fused_computation.11 | loop fusion | flops 4194304 | bytes 16779264 | tf_op jit(solution)/shard_map/jit(_take)/select_n | solution.py:47
  250.8 0.0 all-to-all-done
  250.8 10.4 %all-to-all-start.1 = ((bf16[128,1,16,2048]{3,2,1,0:T(8,128)(2,1)}), bf16[128,1,16,2048]{3,2,1,0:T(8,128)(2,1)}, u32[]{:S(2)}, u32[]{:S(2)}) async-start(bf16[128,1,16,2048]{3,2,1,0:T(8,128)(2,1)} %broadcast_select_fusion), calls=%async_computation.1 | async-start | bytes 16777216 | tf_op jit(solution)/shard_map/all_to_all | solution.py:52
  261.2 4.8 slice_reduce_fusion.1
  266.0 0.2 convert_reduce_fusion
  266.2 6.6 %gather_fusion.4 = s32[1024]{0:T(1024)S(1)} fusion(s32[128]{0:T(128)S(1)} %get-tuple-element.9, s32[1024]{0:T(1024)S(1)} %broadcast_clamp_fusion.4), kind=kCustom, calls=%fused_computation.6 | custom fusion | bytes 12288 | tf_op jit(solution)/shard_map/jit(take_along_axis)/gather | solution.py:60
  272.8 0.1 iota_add_fusion
  272.9 0.1 add.192
  273.0 0.1 iota_compare_fusion.1
  273.1 0.1 lt.210
  273.3 0.1 fusion.36
  273.4 105.8 %all-to-all-done.1 = bf16[128,1,16,2048]{3,2,1,0:T(8,128)(2,1)} async-done(((bf16[128,1,16,2048]{3,2,1,0:T(8,128)(2,1)}), bf16[128,1,16,2048]{3,2,1,0:T(8,128)(2,1)}, u32[]{:S(2)}, u32[]{:S(2)}) %all-to-all-start.1) | async-done | bytes 8388640 | tf_op jit(solution)/shard_map/all_to_all | solution.py:52
  379.2 13.3 %gather_fusion.6 = bf16[1024,2048]{1,0:T(8,128)(2,1)} fusion(bf16[2048,2048]{1,0:T(8,128)(2,1)} %bitcast.14, s32[1024]{0:T(1024)S(1)} %broadcast_clamp_fusion.2), kind=kCustom, calls=%fused_computation.clone | custom fusion | bytes 8392704 | tf_op jit(solution)/shard_map/jit(_take)/gather | solution.py:64
  392.5 0.0 copy-done
  392.5 12.2 %convolution_convert_fusion = bf16[1024,2048]{1,0:T(8,128)(2,1)} fusion(bf16[1,768,2048]{2,1,0:T(8,128)(2,1)S(1)} %copy-done, bf16[1024,2048]{1,0:T(8,128)(2,1)} %gather_fusion.6, pred[1024]{0:T(1024)(128)(4,1)S(1)} %compare_and_fusion.2, bf16[1,2048,768]{2,1,0:T(8,128)(2,1)} %param.10), kind=kOutput, calls=%fused_computation.21 | convolution fusion | flops 6453723136 | bytes 14681088 | tf_op jit(solution)/shard_map/ecf,efd->ecd/dot_general | solution.py:68
  404.7 19.1 %gather_fusion.5 = bf16[2048,2048]{1,0:T(8,128)(2,1)} fusion(bf16[1024,2048]{1,0:T(8,128)(2,1)} %convolution_convert_fusion, s32[2048]{0:T(1024)S(1)} %broadcast_clamp_fusion), kind=kCustom, calls=%fused_computation.7 | custom fusion | bytes 16785408 | tf_op jit(solution)/shard_map/jit(_take)/gather | solution.py:74
  423.8 7.3 %broadcast_select_fusion.1 = bf16[128,1,16,2048]{3,2,1,0:T(8,128)(2,1)} fusion(bf16[128,1,16,2048]{3,2,1,0:T(8,128)(2,1)} %bitcast.50, pred[128,16]{1,0:T(8,128)(4,1)S(1)} %fusion.36), kind=kLoop, calls=%fused_computation.12 | loop fusion | flops 4194304 | bytes 16779264 | tf_op jit(solution)/shard_map/jit(_take)/select_n | solution.py:74
  431.0 0.0 copy-start.3
  431.0 19.3 %all-to-all-start.2 = ((bf16[128,1,16,2048]{3,2,1,0:T(8,128)(2,1)}), bf16[128,1,16,2048]{3,2,1,0:T(8,128)(2,1)}, u32[]{:S(2)}, u32[]{:S(2)}) async-start(bf16[128,1,16,2048]{3,2,1,0:T(8,128)(2,1)} %broadcast_select_fusion.1), calls=%async_computation.2 | async-start | bytes 16777216 | tf_op jit(solution)/shard_map/all_to_all | solution.py:76
  450.4 0.0 copy-done.3
  450.4 0.1 copy.28
  450.5 132.9 %all-to-all-done.2 = bf16[128,1,16,2048]{3,2,1,0:T(8,128)(2,1)} async-done(((bf16[128,1,16,2048]{3,2,1,0:T(8,128)(2,1)}), bf16[128,1,16,2048]{3,2,1,0:T(8,128)(2,1)}, u32[]{:S(2)}, u32[]{:S(2)}) %all-to-all-start.2) | async-done | bytes 8388640 | tf_op jit(solution)/shard_map/all_to_all | solution.py:76
  583.5 13.3 %gather_fusion.7 = bf16[1024,2048]{1,0:T(8,128)(2,1)} fusion(bf16[2048,2048]{1,0:T(8,128)(2,1)} %bitcast.20, s32[1024]{0:T(1024)S(1)} %broadcast_clamp_fusion.1), kind=kCustom, calls=%fused_computation.1.clone | custom fusion | bytes 8392704 | tf_op jit(solution)/shard_map/jit(_take)/gather | solution.py:78
  596.7 0.0 copy-start.2
  596.7 0.0 copy-start.1
  596.7 3.7 fusion
  600.4 0.0 copy-done.2
  600.4 1.1 fusion.24
  601.6 0.0 copy-done.1
  (26 shorter events, 0.2 us)
Async XLA Ops:
  0.0 392.5 %copy-start = (bf16[1,768,2048]{2,1,0:T(8,128)(2,1)S(1)}, bf16[1,768,2048]{2,1,0:T(8,128)(2,1)}, u32[]{:S(2)}) copy-start(bf16[1,768,2048]{2,1,0:T(8,128)(2,1)} %param.11) | copy-start | bytes 9437188
  190.9 59.9 %all-to-all-start = ((s32[128,1,2]{2,1,0:T(1,128)}), s32[128,1,2]{2,1,0:T(1,128)S(1)}, u32[]{:S(2)}, u32[]{:S(2)}) async-start(s32[128,1,2]{2,1,0:T(1,128)} %copy.25), calls=%async_computation | async-start | bytes 131072 | tf_op jit(solution)/shard_map/all_to_all | solution.py:51
  250.8 128.4 %all-to-all-start.1 = ((bf16[128,1,16,2048]{3,2,1,0:T(8,128)(2,1)}), bf16[128,1,16,2048]{3,2,1,0:T(8,128)(2,1)}, u32[]{:S(2)}, u32[]{:S(2)}) async-start(bf16[128,1,16,2048]{3,2,1,0:T(8,128)(2,1)} %broadcast_select_fusion), calls=%async_computation.1 | async-start | bytes 16777216 | tf_op jit(solution)/shard_map/all_to_all | solution.py:52
  431.0 19.4 %copy-start.3 = (f32[128,8]{0,1:T(8,128)S(1)}, f32[128,8]{0,1:T(8,128)}, u32[]{:S(2)}) copy-start(f32[128,8]{0,1:T(8,128)} %param.9) | copy-start | bytes 12292
  431.0 152.4 %all-to-all-start.2 = ((bf16[128,1,16,2048]{3,2,1,0:T(8,128)(2,1)}), bf16[128,1,16,2048]{3,2,1,0:T(8,128)(2,1)}, u32[]{:S(2)}, u32[]{:S(2)}) async-start(bf16[128,1,16,2048]{3,2,1,0:T(8,128)(2,1)} %broadcast_select_fusion.1), calls=%async_computation.2 | async-start | bytes 16777216 | tf_op jit(solution)/shard_map/all_to_all | solution.py:76
  596.7 3.7 copy-start.2
  596.7 4.8 copy-start.1
where the time goes:
time: 605 us; the launch traced here: 602 us
  waiting for transfers between devices  239 us (40%)
  blocking collectives  181 us (30%)
  local copies, waits for them, and re-layouts  103 us (17%)
  starting transfers between devices  33.4 us (6%)
  other arithmetic  28.8 us (5%)
  matrix products  15.9 us (3%)
    all_gather x1, blocking collectives, device_fn(): col_counts = lax.all_gather(counts, 'col')  151 us
    all_to_all x1, waiting for transfers between devices, device_fn(): returned = lax.all_to_all(back_rows, GRID_AXES, 0, 0, tiled=True)  133 us
    all_to_all x1, waiting for transfers between devices, device_fn(): recv_rows = lax.all_to_all(send_rows, GRID_AXES, 0, 0, tiled=True)  106 us
    all_gather x1, blocking collectives, device_fn(): row_totals = lax.all_gather(jnp.sum(col_counts, axis=0), 'row')  30.2 us
    all_to_all x1, starting transfers between devices, device_fn(): returned = lax.all_to_all(back_rows, GRID_AXES, 0, 0, tiled=True)  19.3 us
    gather x1, local copies, waits for them, and re-layouts, device_fn(): jnp.take(expert_out.reshape(-1, model_width), back_index.reshape(-1), axi...  19.1 us
    gather x1, local copies, waits for them, and re-layouts, device_fn(): send_rows = jnp.take(tokens, send_index, axis=0, mode='fill', fill_value=0)  17.4 us
    gather x1, local copies, waits for them, and re-layouts, device_fn(): jnp.take(recv_rows.reshape(-1, model_width), recv_index.reshape(-1), axis...  13.3 us
  transfers between devices with their start and end apart: 3, of which 2 were waited for; matrix products, arithmetic and copies ran while one was open for 11% of the time, Pallas kernels for 0%

commit v1 on v0

v1 whole, which is shorter than its diff:
```python
import functools

import jax
import jax.numpy as jnp
from jax import lax
from jax.experimental import pallas as pl
from jax.experimental.pallas import tpu as pltpu
from jax.sharding import PartitionSpec as P

GRID_AXES = ('row', 'col')
F32 = jnp.float32
BF16 = jnp.bfloat16
I32 = jnp.int32


def kernel(side, cap, slots, tokens_ref, ids_ref, gates_ref, w_in_hbm, w_out_hbm, out_ref,
           w_in, w_out, send, recv, outs, ret, cnt_mine, cnt_all, rank_k, rank_e, gate3, acc,
           w_sem, send_sem, back_sem, cnt_send_sem, cnt_recv_sem, recv_sems, ret_sems):
    plane = side * side
    group = plane
    groups = 2 * side
    n = plane * side * 2
    log = side.bit_length() - 1
    tok, width = tokens_ref.shape
    rows = group * slots
    top = ids_ref.shape[1]

    data = lax.axis_index('data')
    core = lax.axis_index('row')
    col = lax.axis_index('col')
    cz = lax.div(col, plane)
    cy = lax.rem(lax.div(col, side), side)
    cx = lax.rem(col, side)
    me = core * (plane * side) + col

    def steps(k):
        j, m = lax.div(k, group), lax.rem(k, group)
        dc, jj = lax.div(j, side), lax.rem(j, side)
        dy, dx = lax.div(m, side), lax.rem(m, side)
        dz = lax.rem(jj + dx + dy, side)
        return dc, dz, dy, dx

    def ahead(k):
        dc, dz, dy, dx = steps(k)
        to = lax.rem(cz + dz, side) * plane + lax.rem(cy + dy, side) * side + lax.rem(cx + dx, side)
        return (data, lax.rem(core + dc, 2), to)

    def behind(k):
        dc, dz, dy, dx = steps(k)
        to = (lax.rem(cz + side - dz, side) * plane + lax.rem(cy + side - dy, side) * side
              + lax.rem(cx + side - dx, side))
        return (data, lax.rem(core + dc, 2), to)

    def expert_of(k):
        j, m = k >> (2 * log), k & (group - 1)
        dc, jj = j >> log, j & (side - 1)
        dy, dx = m >> log, m & (side - 1)
        dz = (jj + dx + dy) & (side - 1)
        to = ((cz + dz) & (side - 1)) * plane + ((cy + dy) & (side - 1)) * side + ((cx + dx) & (side - 1))
        return ((core + dc) & 1) * (plane * side) + to

    def iota(shape, dim):
        return lax.broadcasted_iota(I32, shape, dim)

    load_in = pltpu.make_async_copy(w_in_hbm, w_in, w_sem.at[0])
    load_out = pltpu.make_async_copy(w_out_hbm, w_out, w_sem.at[1])
    load_in.start()
    load_out.start()

    lane = iota((tok, n), 1)
    chosen = jnp.zeros((tok, n), F32)
    gates = jnp.zeros((tok, n), F32)
    for j in range(top):
        hit = ids_ref[:, j:j + 1] == lane
        chosen = jnp.where(hit, 1.0, chosen)
        gates = jnp.where(hit, gates_ref[:, j:j + 1], gates)
    cnt_mine[...] = jnp.sum(chosen, axis=0, keepdims=True).astype(I32)
    cnt_all[pl.ds(me, 1)] = cnt_mine[...][None]

    @pl.loop(1, n)
    def _(k):
        pltpu.make_async_remote_copy(cnt_mine, cnt_all.at[me], cnt_send_sem, cnt_recv_sem,
                                     device_id=ahead(k), device_id_type=pl.DeviceIdType.MESH).start()

    earlier = (iota((tok, tok), 1) < iota((tok, tok), 0)).astype(BF16)
    rank = jnp.dot(earlier, chosen.astype(BF16), preferred_element_type=F32)
    rank = jnp.where(chosen > 0, rank, -1.0)
    rank_e[...] = rank
    gate3[...] = gates
    order = (expert_of(iota((n, n), 0)) == iota((n, n), 1)).astype(BF16)
    rank_k[...] = lax.dot_general(order, rank.astype(BF16), (((1,), (1,)), ((), ())), preferred_element_type=F32)

    def block_copy(k):
        return pltpu.make_async_remote_copy(send.at[k], recv.at[k], send_sem, recv_sems.at[lax.div(k, group)],
                                            device_id=ahead(k), device_id_type=pl.DeviceIdType.MESH)

    def back_copy(k):
        return pltpu.make_async_remote_copy(outs.at[k], ret.at[k], back_sem, ret_sems.at[lax.div(k, group)],
                                            device_id=behind(k), device_id_type=pl.DeviceIdType.MESH)

    @pl.loop(0, groups)
    def _(j):
        first = j * group
        place = rank_k[pl.ds(first, group), :]
        pick = place[:, None, :] == iota((group, slots, tok), 1).astype(F32)
        pick = jnp.where(pick, 1.0, 0.0).reshape(rows, tok).astype(BF16)
        picked = jnp.dot(pick, tokens_ref[...], preferred_element_type=F32).astype(BF16)
        send[pl.ds(first, group)] = picked.reshape(group, slots, width)

        @pl.loop(jnp.where(j == 0, 1, first), first + group)
        def _(k):
            block_copy(k).start()

    recv[0] = send[0]
    load_in.wait()
    load_out.wait()

    def wait_group(buf, sem, first, count):
        part = buf.at[pl.ds(first, count)]
        pltpu.make_async_copy(part, part, sem).wait()

    def expert(j):
        first = j * group
        x = recv[pl.ds(first, group)].reshape(rows, width)
        hidden = jax.nn.gelu(jnp.dot(x, w_in[...], preferred_element_type=F32)).astype(BF16)
        o = jnp.dot(hidden, w_out[...], preferred_element_type=F32).astype(BF16)
        outs[pl.ds(first, group)] = o.reshape(group, slots, width)

        @pl.loop(jnp.where(j == 0, 1, first), first + group)
        def _(k):
            back_copy(k).start()

    @pl.loop(0, groups)
    def _(j):
        @pl.when(j == 0)
        def _():
            wait_group(recv, recv_sems.at[0], 1, group - 1)

        @pl.when(j > 0)
        def _():
            wait_group(recv, recv_sems.at[j], j * group, group)

        expert(j)

    ret[0] = outs[0]

    wait_group(cnt_all, cnt_recv_sem, 0, n - 1)
    seen = jnp.where(iota((n, 1, n), 0) < me, cnt_all[...], 0)
    before = jnp.sum(seen, axis=0).astype(F32)
    room = jnp.clip(cap - before, 0.0, float(slots))
    rank = rank_e[...]
    rank = jnp.where(rank < room, rank, -1.0)
    gates = gate3[...]
    high = gates.astype(BF16)
    left = gates - high.astype(F32)
    mid = left.astype(BF16)
    low = (left - mid.astype(F32)).astype(BF16)
    parts = jnp.concatenate([high, mid, low], axis=0)
    rank = rank.astype(BF16)
    room_col = jnp.broadcast_to(room, (n, n)).T.astype(BF16)

    acc[...] = tokens_ref[...].astype(F32)

    def combine(j):
        first = j * group
        spread = (expert_of(first + iota((n, rows), 1) // slots) == iota((n, rows), 0)).astype(BF16)
        at = jnp.dot(rank, spread, preferred_element_type=F32)
        here = at == (iota((tok, rows), 1) % slots).astype(F32)
        scale = jnp.dot(parts, spread, preferred_element_type=F32)
        here3 = jnp.concatenate([here.astype(F32)] * 3, axis=0)
        scale = (scale * here3).astype(BF16)
        fits = lax.dot_general(spread, room_col, (((0,), (0,)), ((), ())), preferred_element_type=F32)
        fits = (iota((rows, n), 0) % slots).astype(F32) < fits
        got = ret[pl.ds(first, group)].reshape(rows, width)
        got = jnp.where(fits[:, :1], got, jnp.zeros_like(got))
        mixed = jnp.dot(scale, got, preferred_element_type=F32)
        acc[...] += mixed[:tok] + (mixed[tok:2 * tok] + mixed[2 * tok:])

    @pl.loop(0, groups)
    def _(j):
        @pl.when(j == 0)
        def _():
            wait_group(ret, ret_sems.at[0], 1, group - 1)

        @pl.when(j > 0)
        def _():
            wait_group(ret, ret_sems.at[j], j * group, group)

        combine(j)

    out_ref[...] = acc[...].astype(BF16)
    wait_group(send, send_sem, 1, n - 1)
    wait_group(outs, back_sem, 1, n - 1)

    @pl.loop(1, n)
    def _(k):
        pltpu.make_async_copy(cnt_mine, cnt_mine, cnt_send_sem).wait()


def solution(mesh):
    group_size = mesh.shape['row'] * mesh.shape['col']
    side = round(mesh.shape['col'] ** (1 / 3))

    def device_fn(tokens, expert_ids, gate_weights, w_in, w_out):
        tok, width = tokens.shape
        top = expert_ids.shape[1]
        ff = w_in.shape[2]
        n = group_size
        cap = tok * top
        slots = 2 * tok * top // n
        groups, group = 2 * side, side * side
        vmem = pl.BlockSpec(memory_space=pltpu.VMEM)
        anyspace = pl.BlockSpec(memory_space=pl.ANY)
        blocks = pltpu.VMEM((n, slots, width), BF16)
        return pl.pallas_call(
            functools.partial(kernel, side, cap, slots),
            out_shape=jax.ShapeDtypeStruct((tok, width), BF16),
            in_specs=[vmem, vmem, vmem, anyspace, anyspace],
            out_specs=vmem,
            scratch_shapes=[
                pltpu.VMEM((width, ff), BF16),
                pltpu.VMEM((ff, width), BF16),
                blocks, blocks, blocks, blocks,
                pltpu.VMEM((1, n), I32),
                pltpu.VMEM((n, 1, n), I32),
                pltpu.VMEM((n, tok), F32),
                pltpu.VMEM((tok, n), F32),
                pltpu.VMEM((tok, n), F32),
                pltpu.VMEM((tok, width), F32),
                pltpu.SemaphoreType.DMA((2,)),
                pltpu.SemaphoreType.DMA,
                pltpu.SemaphoreType.DMA,
                pltpu.SemaphoreType.DMA,
                pltpu.SemaphoreType.DMA,
                pltpu.SemaphoreType.DMA((groups,)),
                pltpu.SemaphoreType.DMA((groups,)),
            ],
            compiler_params=pltpu.CompilerParams(has_side_effects=True, vmem_limit_bytes=60 * 1024 * 1024),
            name='expert_layer',
        )(tokens, expert_ids, gate_weights, w_in.reshape(width, ff), w_out.reshape(ff, width))

    token_spec = P(('data', 'row', 'col'), None)
    expert_spec = P(GRID_AXES, None, None)
    return jax.shard_map(device_fn, mesh=mesh, in_specs=(token_spec, token_spec, token_spec, expert_spec, expert_spec), out_specs=token_spec, check_vma=False)
```

time: 605 us -> 286 us (0.47)
  the two profiles are of different devices: /device:TPU:1 before, /device:TPU:17 now
where the time goes in v1:
time: 286 us
  Pallas kernels  281 us (98%)
  local copies, waits for them, and re-layouts  4.7 us (2%)
    pallas_call x1, Pallas kernels, device_fn(): pl.pallas_call(functools.partial(kernel, side, cap, slots), out_shape=jax...  281 us

profile of v1, /device:TPU:17, one launch (start us, length us, event | category | flops | bytes accessed | tf_op | source)
XLA Modules:
  0.0 286.2 jit_solution(5101585117818320883)
XLA Ops:
  0.0 1.4 copy.6.ids_ref
  1.4 1.4 copy.7.gates_ref
  2.8 281.5 %expert_layer.1 = bf16[128,2048]{1,0:T(8,128)(2,1)} custom-call(bf16[128,2048]{1,0:T(8,128)(2,1)} %tokens_ref.1, s32[128,8]{1,0:T(8,128)} %copy.6.ids_ref, f32[128,8]{1,0:T(8,128)} %copy.7.gates_ref, bf16[2048,768]{1,0:T(8,128)(2,1)} %bitcast.2, bf16[768,2048]{1,0:T(8,128)(2,1)} %bitcast.3), custom_call_target="tpu_custom_call" | custom-call | tf_op jit(solution)/shard_map/expert_layer/pallas_call | solution.py:215
  284.3 1.9 copy.9

commit v2 on v0

v2 whole, which is shorter than its diff:
```python
import functools

import jax
import jax.numpy as jnp
from jax import lax
from jax.experimental import pallas as pl
from jax.experimental.pallas import tpu as pltpu
from jax.sharding import PartitionSpec as P

GRID_AXES = ('row', 'col')
F32 = jnp.float32
BF16 = jnp.bfloat16
I32 = jnp.int32
SIDE = 4
N = 2 * SIDE ** 3
MESH = pl.DeviceIdType.MESH
Z, Y, X = 0, 1, 2
AXES = ((Z, Y, X), (Y, X, Z), (X, Z, Y))


def iota(shape, dim):
    return lax.broadcasted_iota(I32, shape, dim)


def kernel(cols, cap, slots, tokens_ref, ids_ref, gates_ref, ids_t_ref, w_in_hbm, w_out_hbm, out_ref,
           w_in, w_out, tok0, tok1, tok2, blk0, blk1, blk2, recv, ret, ids_all, places,
           cnt_mine, cnt_all, rank_e, gate_e, acc,
           w_sem, ids_send, ids_recv, cnt_send, cnt_recv, tok_send_a, tok_send_b, tok_recv, blk_send, blk_recv, back_send, ret_recv):
    toks, blks = (tok0, tok1, tok2), (blk0, blk1, blk2)
    tok, width = tokens_ref.shape
    top = ids_ref.shape[1]
    data = lax.axis_index('data')
    core = lax.axis_index('row')
    col = lax.axis_index('col')
    here = (lax.div(col, 16), lax.rem(lax.div(col, 4), 4), lax.rem(col, 4))
    me = core * 64 + col

    def device(d_core, d):
        at = [lax.rem(here[a] + d[a], 4) if a in d else here[a] for a in range(3)]
        return (data, lax.rem(core + d_core, 2), at[0] * 16 + at[1] * 4 + at[2])

    def part(p):
        return pl.ds(cols[p][0], cols[p][1])

    load_in = pltpu.make_async_copy(w_in_hbm, w_in, w_sem.at[0])
    load_out = pltpu.make_async_copy(w_out_hbm, w_out, w_sem.at[1])

    cnt_lane = iota((tok, N), 1)
    chosen = jnp.zeros((tok, N), F32)
    gates = jnp.zeros((tok, N), F32)
    for j in range(top):
        hit = ids_ref[:, j:j + 1] == cnt_lane
        chosen = jnp.where(hit, 1.0, chosen)
        gates = jnp.where(hit, gates_ref[:, j:j + 1], gates)
    cnt_mine[...] = jnp.sum(chosen, axis=0, keepdims=True).astype(I32)
    cnt_all[pl.ds(me, 1)] = cnt_mine[...][None]

    for p in range(3):
        d1, d2, d3 = AXES[p]

        @pl.loop(1, 16)
        def _(i):
            pltpu.make_async_remote_copy(
                ids_t_ref, ids_all.at[p, i], ids_send.at[p], ids_recv.at[p],
                device_id=device(0, {d2: lax.div(i, 4), d1: lax.rem(i, 4)}), device_id_type=MESH).start()

    def token_copy(p, src, dst, sem, axis, step, send_sem):
        return pltpu.make_async_remote_copy(src, dst, send_sem.at[p], sem, device_id=device(0, {axis: step}), device_id_type=MESH)

    for p in range(3):
        mine = tokens_ref.at[:, part(p)]
        for step in (1, 3):
            token_copy(p, mine, toks[p].at[0, step], tok_recv.at[p, step], AXES[p][0], step, tok_send_a).start()

    def gather_on(p, a, src):
        for step in (1, 3):
            token_copy(p, src, toks[p].at[step, a], tok_recv.at[p, 4 * step + a], AXES[p][1], step, tok_send_b).start()

    for p in range(3):
        gather_on(p, 0, tokens_ref.at[:, part(p)])

    @pl.loop(1, N)
    def _(k):
        pltpu.make_async_remote_copy(
            cnt_mine, cnt_all.at[me], cnt_send, cnt_recv,
            device_id=device(lax.div(k, 64), {Z: lax.rem(lax.div(k, 16), 4), Y: lax.rem(lax.div(k, 4), 4), X: lax.rem(k, 4)}),
            device_id_type=MESH).start()

    load_in.start()
    load_out.start()

    def wait_for(ref, sem):
        pltpu.make_async_copy(ref, ref, sem).wait()

    def arrived(p, b, a):
        wait_for(toks[p].at[b, a], tok_recv.at[p, 4 * b + a])

    for p in range(3):
        toks[p][0, 0] = tokens_ref[:, part(p)]
        ids_all[p, 0] = ids_t_ref[...]

    earlier = (iota((tok, tok), 1) < iota((tok, tok), 0)).astype(BF16)
    rank = jnp.dot(earlier, chosen.astype(BF16), preferred_element_type=F32)
    rank_e[...] = jnp.where(chosen > 0, rank, -1.0)
    gate_e[...] = gates

    half = tok // 2
    for p in range(3):
        t = toks[p]
        for step, rows in ((1, pl.ds(0, half)), (3, pl.ds(half, half))):
            arrived(p, 0, step)
            token_copy(p, t.at[0, step, rows], t.at[0, 2, rows], tok_recv.at[p, 2], AXES[p][0], step, tok_send_a).start()
            gather_on(p, step, t.at[0, step])

    later = (iota((tok, tok), 0) < iota((tok, tok), 1)).astype(BF16)
    for p in range(3):
        d1, d2, d3 = AXES[p]
        wait_for(ids_all.at[p, pl.ds(1, 15)], ids_recv.at[p])
        dest = iota((8, tok), 0)
        weight = (16, 4, 1)[d3]
        expert = (((core + (dest >> 2)) & 1) * 64 + col + (((here[d3] + (dest & 3)) & 3) - here[d3]) * weight)[None]
        mark = jnp.zeros((16, 8, tok), F32)
        for j in range(top):
            mark = jnp.where(ids_all[p, :, j:j + 1, :] == expert, 1.0, mark)
        mark = mark.reshape(128, tok)
        place = jnp.dot(mark.astype(BF16), later, preferred_element_type=F32)
        places[p] = jnp.where(mark > 0, place, -1.0)

    for p in range(3):
        arrived(p, 0, 2)
        gather_on(p, 2, toks[p].at[0, 2])

    def where_in(p, d_core, s1, s2, s3):
        at = [None] * 3
        for axis, s in zip(AXES[p], (s1, s2, s3)):
            at[axis] = s
        return (d_core, *at)

    def build(p, b):
        t, blk = toks[p], blks[p]

        @pl.loop(0, 4)
        def _(a):
            place = places[p, pl.ds((4 * b + a) * 8, 8), :]
            pick = place[:, None, :] == iota((8, slots, tok), 1).astype(F32)
            pick = jnp.where(pick, 1.0, 0.0).reshape(8 * slots, tok).astype(BF16)
            rows = jnp.dot(pick, t[b, a], preferred_element_type=F32).astype(BF16).reshape(8, slots, cols[p][1])
            blk[b, :, a] = rows
            recv[where_in(p, 0, a, b, 0) + (slice(None), part(p))] = rows[0]

        for h in range(2):
            @pl.loop(1, 8)
            def _(d):
                d_core, s3 = lax.div(d, 4), lax.rem(d, 4)
                high = {AXES[p][0]: h, AXES[p][1]: b // 2, AXES[p][2]: lax.div(s3, 2)}
                cube = high[Z] * 4 + high[Y] * 2 + high[X]
                pltpu.make_async_remote_copy(
                    blk.at[b, d, pl.ds(2 * h, 2)],
                    recv.at[where_in(p, d_core, pl.ds(2 * h, 2), b, s3) + (slice(None), part(p))],
                    blk_send.at[p], blk_recv.at[p, cube],
                    device_id=device(d_core, {AXES[p][2]: s3}), device_id_type=MESH).start()

    for p in range(3):
        build(p, 0)

    for p in range(3):
        t = toks[p]
        for step, pieces in ((1, (0, 1)), (3, (3, 2))):
            for a in pieces:
                arrived(p, step, a)
                token_copy(p, t.at[step, a], t.at[2, a], tok_recv.at[p, 8 + a], AXES[p][1], step, tok_send_b).start()

    for step, rest in ((1, (3, 2)), (3, (0, 1))):
        for p in range(3):
            for a in rest:
                arrived(p, step, a)
            build(p, step)

    load_in.wait()
    load_out.wait()

    def expert(j):
        hz, hy, hx = lax.div(j, 4), lax.rem(lax.div(j, 2), 2), lax.rem(j, 2)
        cube = (slice(None), pl.ds(2 * hz, 2), pl.ds(2 * hy, 2), pl.ds(2 * hx, 2))
        x = recv[cube].reshape(16 * slots, width)
        hidden = jax.nn.gelu(jnp.dot(x, w_in[...], preferred_element_type=F32)).astype(BF16)
        o = jnp.dot(hidden, w_out[...], preferred_element_type=F32).astype(BF16)
        recv[cube] = o.reshape(2, 2, 2, 2, slots, width)

        @pl.loop(jnp.where(j == 0, 1, 0), 16)
        def _(i):
            d_core = lax.div(i, 8)
            sz = 2 * hz + lax.rem(lax.div(i, 4), 2)
            sy = 2 * hy + lax.rem(lax.div(i, 2), 2)
            sx = 2 * hx + lax.rem(i, 2)
            pltpu.make_async_remote_copy(
                recv.at[d_core, sz, sy, sx], ret.at[j * 16 + i], back_send, ret_recv.at[j],
                device_id=device(d_core, {Z: 4 - sz, Y: 4 - sy, X: 4 - sx}), device_id_type=MESH).start()

    def wait_cube(j):
        high = (j // 4, (j // 2) % 2, j % 2)
        for p in range(3):
            near = high[AXES[p][2]] == 0
            wait_for(blks[p].at[0, pl.ds(0, 3 if near else 4)], blk_recv.at[p, j])

    wait_cube(0)
    expert(0)
    ret[0] = recv[0, 0, 0, 0]

    for p in range(3):
        for a in range(4):
            arrived(p, 2, a)
        build(p, 2)

    for j in range(1, 8):
        wait_cube(j)
    pl.loop(1, 8)(expert)

    wait_for(cnt_all.at[pl.ds(0, N - 1)], cnt_recv)
    before = jnp.sum(jnp.where(iota((N, 1, N), 0) < me, cnt_all[...], 0), axis=0).astype(F32)
    room = jnp.clip(cap - before, 0.0, float(slots))
    rank = rank_e[...]
    rank = jnp.where(rank < room, rank, -1.0).astype(BF16)
    gates = gate_e[...]
    high = gates.astype(BF16)
    left = gates - high.astype(F32)
    mid = left.astype(BF16)
    low = (left - mid.astype(F32)).astype(BF16)
    thirds = jnp.concatenate([high, mid, low], axis=0)
    room_col = jnp.broadcast_to(room, (N, N)).T.astype(BF16)
    acc[...] = tokens_ref[...].astype(F32)
    rows = 16 * slots

    def combine(j):
        i = iota((N, rows), 1) // slots
        hz, hy, hx = lax.div(j, 4), lax.rem(lax.div(j, 2), 2), lax.rem(j, 2)
        there = (((core + (i >> 3)) & 1) * 64 + ((here[Z] + 2 * hz + ((i >> 2) & 1)) & 3) * 16
                 + ((here[Y] + 2 * hy + ((i >> 1) & 1)) & 3) * 4 + ((here[X] + 2 * hx + (i & 1)) & 3))
        spread = (there == iota((N, rows), 0)).astype(BF16)
        at = jnp.dot(rank, spread, preferred_element_type=F32)
        hit = (at == (iota((tok, rows), 1) % slots).astype(F32)).astype(F32)
        scale = jnp.dot(thirds, spread, preferred_element_type=F32)
        scale = (scale * jnp.concatenate([hit] * 3, axis=0)).astype(BF16)
        fits = lax.dot_general(spread, room_col, (((0,), (0,)), ((), ())), preferred_element_type=F32)
        fits = (iota((rows, N), 0) % slots).astype(F32) < fits
        got = ret[pl.ds(16 * j, 16)].reshape(rows, width)
        got = jnp.where(fits[:, :1], got, jnp.zeros_like(got))
        mixed = jnp.dot(scale, got, preferred_element_type=F32)
        acc[...] += mixed[:tok] + (mixed[tok:2 * tok] + mixed[2 * tok:])

    @pl.loop(0, 8)
    def _(j):
        @pl.when(j == 0)
        def _():
            wait_for(ret.at[pl.ds(1, 15)], ret_recv.at[0])

        @pl.when(j > 0)
        def _():
            wait_for(ret.at[pl.ds(16 * j, 16)], ret_recv.at[j])

        combine(j)

    out_ref[...] = acc[...].astype(BF16)

    wait_for(ret.at[pl.ds(1, N - 1)], back_send)
    wait_for(cnt_all.at[pl.ds(0, N - 1)], cnt_send)
    for p in range(3):
        wait_for(blks[p].at[:, pl.ds(1, 7)], blk_send.at[p])
        wait_for(ids_all.at[p, pl.ds(1, 15)], ids_send.at[p])
        wait_for(toks[p].at[0, pl.ds(0, 3)], tok_send_a.at[p])
        wait_for(toks[p].at[pl.ds(0, 3)], tok_send_b.at[p])


def solution(mesh):
    def device_fn(tokens, expert_ids, gate_weights, w_in, w_out):
        tok, width = tokens.shape
        top = expert_ids.shape[1]
        ff = w_in.shape[2]
        cap = tok * top
        slots = 2 * tok * top // N
        tiles = width // 128
        sizes = [128 * (tiles // 3 + (1 if p < tiles % 3 else 0)) for p in range(3)]
        cols = [(sum(sizes[:p]), sizes[p]) for p in range(3)]
        vmem = pl.BlockSpec(memory_space=pltpu.VMEM)
        anyspace = pl.BlockSpec(memory_space=pl.ANY)
        dma = pltpu.SemaphoreType.DMA
        return pl.pallas_call(
            functools.partial(kernel, cols, cap, slots),
            out_shape=jax.ShapeDtypeStruct((tok, width), BF16),
            in_specs=[vmem, vmem, vmem, vmem, anyspace, anyspace],
            out_specs=vmem,
            scratch_shapes=[
                pltpu.VMEM((width, ff), BF16),
                pltpu.VMEM((ff, width), BF16),
                *[pltpu.VMEM((4, 4, tok, s), BF16) for s in sizes],
                *[pltpu.VMEM((4, 8, 4, slots, s), BF16) for s in sizes],
                pltpu.VMEM((2, 4, 4, 4, slots, width), BF16),
                pltpu.VMEM((N, slots, width), BF16),
                pltpu.VMEM((3, 16, top, tok), I32),
                pltpu.VMEM((3, 128, tok), F32),
                pltpu.VMEM((1, N), I32),
                pltpu.VMEM((N, 1, N), I32),
                pltpu.VMEM((tok, N), F32),
                pltpu.VMEM((tok, N), F32),
                pltpu.VMEM((tok, width), F32),
                dma((2,)), dma((3,)), dma((3,)), dma, dma, dma((3,)), dma((3,)), dma((3, 16)),
                dma((3,)), dma((3, 8)), dma, dma((8,)),
            ],
            compiler_params=pltpu.CompilerParams(has_side_effects=True, vmem_limit_bytes=62 * 1024 * 1024),
            name='expert_layer',
        )(tokens, expert_ids, gate_weights, expert_ids.T, w_in.reshape(width, ff), w_out.reshape(ff, width))

    token_spec = P(('data', 'row', 'col'), None)
    expert_spec = P(GRID_AXES, None, None)
    return jax.shard_map(device_fn, mesh=mesh, in_specs=(token_spec, token_spec, token_spec, expert_spec, expert_spec), out_specs=token_spec, check_vma=False)
```

time: 605 us -> 234 us (0.39)
  the two profiles are of different devices: /device:TPU:1 before, /device:TPU:36 now
where the time goes in v2:
time: 234 us; the launch traced here: 233 us
  Pallas kernels  229 us (98%)
  local copies, waits for them, and re-layouts  4.7 us (2%)
    pallas_call x1, Pallas kernels, device_fn(): pl.pallas_call(functools.partial(kernel, cols, cap, slots), out_shape=jax...  229 us
    unnamed x3, local copies, waits for them, and re-layouts  4.7 us

profile of v2, /device:TPU:36, one launch (start us, length us, event | category | flops | bytes accessed | tf_op | source)
XLA Modules:
  0.0 233.4 jit_solution(8985603795836135169)
XLA Ops:
  0.0 1.4 copy.7.gates_ref
  1.4 1.4 copy.6.ids_ref
  2.8 228.7 %expert_layer.1 = bf16[128,2048]{1,0:T(8,128)(2,1)} custom-call(bf16[128,2048]{1,0:T(8,128)(2,1)} %tokens_ref.1, s32[128,8]{1,0:T(8,128)} %copy.6.ids_ref, f32[128,8]{1,0:T(8,128)} %copy.7.gates_ref, s32[8,128]{1,0:T(8,128)} %bitcast.5, bf16[2048,768]{1,0:T(8,128)(2,1)} %bitcast.3, bf16[768,2048]{1,0:T(8,128)(2,1)} %bitcast.4), custom_call_target="tpu_custom_call" | custom-call | tf_op jit(solution)/shard_map/expert_layer/pallas_call | solution.py:287
  231.6 1.9 copy.9

commit v3 on v2

v3 whole, which is shorter than its diff:
```python
import functools

import jax
import jax.numpy as jnp
from jax import lax
from jax.experimental import pallas as pl
from jax.experimental.pallas import tpu as pltpu
from jax.sharding import PartitionSpec as P

GRID_AXES = ('row', 'col')
F32 = jnp.float32
BF16 = jnp.bfloat16
I32 = jnp.int32
SIDE = 4
N = 2 * SIDE ** 3
MESH = pl.DeviceIdType.MESH
Z, Y, X = 0, 1, 2
AXES = ((Z, Y, X), (Y, X, Z), (X, Z, Y))


def iota(shape, dim):
    return lax.broadcasted_iota(I32, shape, dim)


def kernel(cols, cap, slots, tokens_ref, ids_ref, gates_ref, w_in_hbm, w_out_hbm, out_ref,
           w_in, w_out, tok0, tok1, tok2, blk0, blk1, blk2, recv, mid0, mid1, mid2, end0, end1, end2,
           sum0, sum1, sum2, got0, got1, got2, ids_all, gates_all, places, cnt_mine, cnt_all, acc,
           w_sem, ids_send, ids_recv, gate_send, gate_recv, cnt_send, cnt_recv, tok_send_a, tok_send_b, tok_recv,
           blk_send, blk_recv, mid_send, mid_recv, end_send, end_recv, sum_send, sum_recv):
    toks, blks = (tok0, tok1, tok2), (blk0, blk1, blk2)
    mids, ends = (mid0, mid1, mid2), (end0, end1, end2)
    sums, gots = (sum0, sum1, sum2), (got0, got1, got2)
    tok, width = tokens_ref.shape
    top = ids_ref.shape[0]
    data = lax.axis_index('data')
    core = lax.axis_index('row')
    col = lax.axis_index('col')
    here = (lax.div(col, 16), lax.rem(lax.div(col, 4), 4), lax.rem(col, 4))
    me = core * 64 + col
    weight = (16, 4, 1)

    def device(d_core, d):
        at = [lax.rem(here[a] + d[a], 4) if a in d else here[a] for a in range(3)]
        return (data, lax.rem(core + d_core, 2), at[0] * 16 + at[1] * 4 + at[2])

    def number(d_core, d):
        n = ((core + d_core) & 1) * 64
        for a in range(3):
            n = n + (((here[a] + d[a]) & 3) if a in d else here[a]) * weight[a]
        return n

    def part(p):
        return pl.ds(cols[p][0], cols[p][1])

    def send(src, dst, send_sem, recv_sem, to):
        pltpu.make_async_remote_copy(src, dst, send_sem, recv_sem, device_id=to, device_id_type=MESH).start()

    def wait_for(ref, sem):
        pltpu.make_async_copy(ref, ref, sem).wait()

    load_in = pltpu.make_async_copy(w_in_hbm, w_in, w_sem.at[0])
    load_out = pltpu.make_async_copy(w_out_hbm, w_out, w_sem.at[1])

    for p in range(3):
        for step in (1, 3):
            send(tokens_ref.at[:, part(p)], toks[p].at[0, step], tok_send_a.at[p], tok_recv.at[p, step], device(0, {AXES[p][0]: step}))

    mark = jnp.zeros((N, tok), F32)
    for j in range(top):
        mark = jnp.where(ids_ref[j:j + 1, :] == iota((N, tok), 0), 1.0, mark)
    counts = lax.dot_general(jnp.ones((8, tok), BF16), mark.astype(BF16), (((1,), (1,)), ((), ())), preferred_element_type=F32)
    cnt_mine[...] = counts[:1]
    cnt_all[pl.ds(me, 1)] = counts[:1][None]

    @pl.loop(1, N)
    def _(k):
        d = {Z: lax.rem(lax.div(k, 16), 4), Y: lax.rem(lax.div(k, 4), 4), X: lax.rem(k, 4)}
        send(cnt_mine, cnt_all.at[me], cnt_send, cnt_recv, device(lax.div(k, 64), d))

    for p in range(3):
        d1, d2, d3 = AXES[p]

        @pl.loop(1, 16)
        def _(i):
            send(ids_ref, ids_all.at[p, i], ids_send.at[p], ids_recv.at[p], device(0, {d2: lax.div(i, 4), d1: lax.rem(i, 4)}))

        @pl.loop(1, 4)
        def _(i):
            send(gates_ref, gates_all.at[p, i], gate_send.at[p], gate_recv.at[p], device(0, {d1: i}))

    def gather_on(p, a, src):
        for step in (1, 3):
            send(src, toks[p].at[step, a], tok_send_b.at[p], tok_recv.at[p, 4 * step + a], device(0, {AXES[p][1]: step}))

    for p in range(3):
        gather_on(p, 0, tokens_ref.at[:, part(p)])

    load_in.start()
    load_out.start()

    def arrived(p, b, a):
        wait_for(toks[p].at[b, a], tok_recv.at[p, 4 * b + a])

    for p in range(3):
        toks[p][0, 0] = tokens_ref[:, part(p)]
        ids_all[p, 0] = ids_ref[...]
        gates_all[p, 0] = gates_ref[...]

    half = tok // 2
    for p in range(3):
        t = toks[p]
        for step, rows in ((1, pl.ds(0, half)), (3, pl.ds(half, half))):
            arrived(p, 0, step)
            send(t.at[0, step, rows], t.at[0, 2, rows], tok_send_a.at[p], tok_recv.at[p, 2], device(0, {AXES[p][0]: step}))
            gather_on(p, step, t.at[0, step])

    wait_for(cnt_all.at[pl.ds(0, N - 1)], cnt_recv)
    below = (iota((N, N), 1) < iota((N, N), 0)).astype(BF16)
    before = jnp.dot(below, jnp.sum(cnt_all[...], axis=1).astype(BF16), preferred_element_type=F32)
    room = jnp.clip(cap - before, 0.0, float(slots)).astype(BF16)

    later = (iota((tok, tok), 0) < iota((tok, tok), 1)).astype(BF16)
    for p in range(3):
        d1, d2, d3 = AXES[p]
        wait_for(ids_all.at[p, pl.ds(1, 15)], ids_recv.at[p])
        dest = iota((8, tok), 0)
        expert_id = number(dest >> 2, {d3: dest & 3})[None]
        mark = jnp.zeros((16, 8, tok), F32)
        for j in range(top):
            mark = jnp.where(ids_all[p, :, j:j + 1, :] == expert_id, 1.0, mark)
        mark = mark.reshape(128, tok)
        place = jnp.dot(mark.astype(BF16), later, preferred_element_type=F32)
        i = iota((128, N), 0)
        source = number(0, {d2: 4 - (i >> 5), d1: 4 - ((i >> 3) & 3)})
        mine = jnp.dot((source == iota((128, N), 1)).astype(BF16), room, preferred_element_type=F32)
        target = number((i >> 2) & 1, {d3: i & 3})
        mine = jnp.sum(jnp.where(target == iota((128, N), 1), mine, 0.0), axis=1, keepdims=True)
        places[p] = jnp.where((mark > 0) & (place < mine), place, -1.0)

    for p in range(3):
        arrived(p, 0, 2)
        gather_on(p, 2, toks[p].at[0, 2])

    def where_in(p, d_core, s1, s2, s3):
        at = [None] * 3
        for axis, s in zip(AXES[p], (s1, s2, s3)):
            at[axis] = s
        return (d_core, *at)

    def build(p, b):
        t, blk = toks[p], blks[p]

        @pl.loop(0, 4)
        def _(a):
            place = places[p, pl.ds((4 * b + a) * 8, 8), :]
            pick = place[:, None, :] == iota((8, slots, tok), 1).astype(F32)
            pick = jnp.where(pick, 1.0, 0.0).reshape(8 * slots, tok).astype(BF16)
            rows = jnp.dot(pick, t[b, a], preferred_element_type=F32).astype(BF16).reshape(8, slots, cols[p][1])
            blk[b, :, a] = rows
            recv[where_in(p, 0, a, b, 0) + (slice(None), part(p))] = rows[0]

        for h in range(2):
            @pl.loop(1, 8)
            def _(d):
                d_core, s3 = lax.div(d, 4), lax.rem(d, 4)
                high = {AXES[p][0]: h, AXES[p][1]: b // 2, AXES[p][2]: lax.div(s3, 2)}
                cube = high[Z] * 4 + high[Y] * 2 + high[X]
                send(blk.at[b, d, pl.ds(2 * h, 2)],
                     recv.at[where_in(p, d_core, pl.ds(2 * h, 2), b, s3) + (slice(None), part(p))],
                     blk_send.at[p], blk_recv.at[p, cube], device(d_core, {AXES[p][2]: s3}))

    for p in range(3):
        build(p, 0)

    for p in range(3):
        t = toks[p]
        for step, pieces in ((1, (0, 1)), (3, (3, 2))):
            for a in pieces:
                arrived(p, step, a)
                send(t.at[step, a], t.at[2, a], tok_send_b.at[p], tok_recv.at[p, 8 + a], device(0, {AXES[p][1]: step}))

    for step, rest in ((1, (3, 2)), (3, (0, 1))):
        for p in range(3):
            for a in rest:
                arrived(p, step, a)
            build(p, step)

    load_in.wait()
    load_out.wait()

    def halves(j):
        return (lax.div(j, 4), lax.rem(lax.div(j, 2), 2), lax.rem(j, 2))

    def wait_blocks(p, h3, refs, sem):
        @pl.when(h3 == 0)
        def _():
            wait_for(refs.at[0, pl.ds(0, 3)], sem)

        @pl.when(h3 == 1)
        def _():
            wait_for(refs.at[0, pl.ds(0, 4)], sem)

    def expert(j):
        high = halves(j)
        pair = [pl.ds(2 * h, 2) for h in high]
        for p in range(3):
            wait_blocks(p, high[AXES[p][2]], blks[p], blk_recv.at[p, j])
        cube = (slice(None), *pair)
        x = recv[cube].reshape(16 * slots, width)
        hidden = jax.nn.gelu(jnp.dot(x, w_in[...], preferred_element_type=F32)).astype(BF16)
        o = jnp.dot(hidden, w_out[...], preferred_element_type=F32).astype(BF16)
        recv[cube] = o.reshape(2, 2, 2, 2, slots, width)

        for p in range(3):
            d3 = AXES[p][2]
            rest = [pair[a] for a in range(3) if a != d3]

            def along(s3):
                return tuple(s3 if a == d3 else pair[a] for a in range(3))

            @pl.when(high[d3] == 0)
            def _():
                mids[p][(*rest, 0)] = recv[(0, *along(0), slice(None), part(p))]

            @pl.loop(jnp.where(high[d3] == 0, 1, 0), 4)
            def _(i):
                d_core, s3 = lax.div(i, 2), 2 * high[d3] + lax.rem(i, 2)
                send(recv.at[(d_core, *along(s3), slice(None), part(p))], mids[p].at[(*rest, d_core * 4 + s3)],
                     mid_send.at[p], mid_recv.at[p, j], device(d_core, {d3: 4 - s3}))

    def middle(p, s1, s2):
        d1, d2 = AXES[p][:2]
        return (s1, s2) if d1 < d2 else (s2, s1)

    def pass_on(j):
        high = halves(j)
        for p in range(3):
            d1, d2, d3 = AXES[p]

            @pl.when(high[d3] == 1)
            def _():
                wait_blocks(p, 0, blks[p], mid_recv.at[p, j - (4, 2, 1)[d3]])
                wait_blocks(p, 1, blks[p], mid_recv.at[p, j])
                first = pl.ds(2 * high[d1], 2)

                @pl.when(high[d2] == 0)
                def _():
                    ends[p][first, 0] = mids[p][middle(p, first, 0)]

                @pl.loop(jnp.where(high[d2] == 0, 1, 2 * high[d2]), 2 * high[d2] + 2)
                def _(s2):
                    send(mids[p].at[middle(p, first, s2)], ends[p].at[first, s2],
                         end_send.at[p], end_recv.at[p, high[d1]], device(0, {d2: 4 - s2}))

    def combine(p, h):
        d1, d2, d3 = AXES[p]
        e = iota((32, tok), 0)
        expert_id = number((e >> 2) & 1, {d2: e >> 3, d3: e & 3})
        scales = []
        for s1 in (2 * h, 2 * h + 1):
            mark = jnp.zeros((32, tok), F32)
            gate = jnp.zeros((32, tok), F32)
            for j in range(top):
                hit = ids_all[p, s1, j:j + 1, :] == expert_id
                mark = jnp.where(hit, 1.0, mark)
                gate = jnp.where(hit, gates_all[p, s1, j:j + 1, :], gate)
            place = jnp.dot(mark.astype(BF16), later, preferred_element_type=F32)
            place = jnp.where(mark > 0, place, -1.0)
            scale = jnp.where(place[:, None, :] == iota((32, slots, tok), 1).astype(F32), gate[:, None, :], 0.0)
            scale = scale.reshape(32 * slots, tok).T
            high = scale.astype(BF16)
            left = scale - high.astype(F32)
            mid = left.astype(BF16)
            low = (left - mid.astype(F32)).astype(BF16)
            scales.append(jnp.concatenate([high, mid, low], axis=0))
        wait_for(ends[p].at[pl.ds(2 * h, 2), pl.ds(1, 3)], end_recv.at[p, h])
        for s1 in (2 * h, 2 * h + 1):
            rows = ends[p][s1].reshape(32 * slots, cols[p][1])
            mixed = jnp.dot(scales[s1 - 2 * h], rows, preferred_element_type=F32)
            mixed = mixed[:tok] + (mixed[tok:2 * tok] + mixed[2 * tok:])
            if s1 == 0:
                acc[:, part(p)] = tokens_ref[:, part(p)].astype(F32) + mixed
            else:
                sums[p][s1 - 1] = mixed
                send(sums[p].at[s1 - 1], gots[p].at[s1 - 1], sum_send.at[p], sum_recv.at[p, s1 - 1], device(0, {d1: 4 - s1}))

    pl.loop(0, 1)(expert)

    for p in range(3):
        for a in range(4):
            arrived(p, 2, a)
        build(p, 2)

    for p in range(3):
        wait_for(gates_all.at[p, pl.ds(1, 3)], gate_recv.at[p])

    @pl.loop(1, 8)
    def _(j):
        expert(j)
        pass_on(j - 1)

    pl.loop(7, 8)(pass_on)
    for h in range(2):
        for p in range(3):
            combine(p, h)

    for p in range(3):
        total = acc[:, part(p)]
        for i in range(3):
            wait_for(gots[p].at[i], sum_recv.at[p, i])
            total = total + gots[p][i]
        out_ref[:, part(p)] = total.astype(BF16)

    wait_for(cnt_all.at[pl.ds(0, N - 1)], cnt_send)
    for p in range(3):
        wait_for(ids_all.at[p, pl.ds(1, 15)], ids_send.at[p])
        wait_for(gates_all.at[p, pl.ds(1, 3)], gate_send.at[p])
        wait_for(toks[p].at[0, pl.ds(0, 3)], tok_send_a.at[p])
        wait_for(toks[p].at[pl.ds(0, 3)], tok_send_b.at[p])
        wait_for(blks[p].at[:, pl.ds(1, 7)], blk_send.at[p])
        wait_for(mids[p].at[:, :, pl.ds(1, 7)], mid_send.at[p])
        wait_for(ends[p].at[:, pl.ds(1, 3)], end_send.at[p])
        wait_for(sums[p], sum_send.at[p])


def solution(mesh):
    def device_fn(tokens, expert_ids, gate_weights, w_in, w_out):
        tok, width = tokens.shape
        top = expert_ids.shape[1]
        ff = w_in.shape[2]
        cap = tok * top
        slots = 2 * tok * top // N
        tiles = width // 128
        sizes = [128 * (tiles // 3 + (1 if p < tiles % 3 else 0)) for p in range(3)]
        cols = [(sum(sizes[:p]), sizes[p]) for p in range(3)]
        vmem = pl.BlockSpec(memory_space=pltpu.VMEM)
        anyspace = pl.BlockSpec(memory_space=pl.ANY)
        dma = pltpu.SemaphoreType.DMA
        return pl.pallas_call(
            functools.partial(kernel, cols, cap, slots),
            out_shape=jax.ShapeDtypeStruct((tok, width), BF16),
            in_specs=[vmem, vmem, vmem, anyspace, anyspace],
            out_specs=vmem,
            scratch_shapes=[
                pltpu.VMEM((width, ff), BF16),
                pltpu.VMEM((ff, width), BF16),
                *[pltpu.VMEM((4, 4, tok, s), BF16) for s in sizes],
                *[pltpu.VMEM((4, 8, 4, slots, s), BF16) for s in sizes],
                pltpu.VMEM((2, 4, 4, 4, slots, width), BF16),
                *[pltpu.VMEM((4, 4, 8, slots, s), BF16) for s in sizes],
                *[pltpu.VMEM((4, 4, 8, slots, s), BF16) for s in sizes],
                *[pltpu.VMEM((3, tok, s), F32) for s in sizes],
                *[pltpu.VMEM((3, tok, s), F32) for s in sizes],
                pltpu.VMEM((3, 16, top, tok), I32),
                pltpu.VMEM((3, 4, top, tok), F32),
                pltpu.VMEM((3, 128, tok), F32),
                pltpu.VMEM((1, N), F32),
                pltpu.VMEM((N, 1, N), F32),
                pltpu.VMEM((tok, width), F32),
                dma((2,)), dma((3,)), dma((3,)), dma((3,)), dma((3,)), dma, dma, dma((3,)), dma((3,)), dma((3, 16)),
                dma((3,)), dma((3, 8)), dma((3,)), dma((3, 8)), dma((3,)), dma((3, 2)), dma((3,)), dma((3, 3)),
            ],
            compiler_params=pltpu.CompilerParams(has_side_effects=True, vmem_limit_bytes=67043328),
            name='expert_layer',
        )(tokens, expert_ids.T, gate_weights.T, w_in.reshape(width, ff), w_out.reshape(ff, width))

    token_spec = P(('data', 'row', 'col'), None)
    expert_spec = P(GRID_AXES, None, None)
    return jax.shard_map(device_fn, mesh=mesh, in_specs=(token_spec, token_spec, token_spec, expert_spec, expert_spec), out_specs=token_spec, check_vma=False)
```

time: 234 us -> 186 us (0.79)
  the two profiles are of different devices: /device:TPU:36 before, /device:TPU:1 now
where the time goes in v3:
time: 186 us
  Pallas kernels  184 us (99%)
  local copies, waits for them, and re-layouts  1.88 us (1%)
    pallas_call x1, Pallas kernels, device_fn(): pl.pallas_call(functools.partial(kernel, cols, cap, slots), out_shape=jax...  184 us

profile of v3, /device:TPU:1, one launch (start us, length us, event | category | flops | bytes accessed | tf_op | source)
XLA Modules:
  0.0 185.8 jit_solution(5008644533409202877)
XLA Ops:
  0.0 183.9 %expert_layer.1 = bf16[128,2048]{1,0:T(8,128)(2,1)} custom-call(bf16[128,2048]{1,0:T(8,128)(2,1)} %tokens_ref.1, s32[8,128]{1,0:T(8,128)} %bitcast.6, f32[8,128]{1,0:T(8,128)} %bitcast.7, bf16[2048,768]{1,0:T(8,128)(2,1)} %bitcast.4, bf16[768,2048]{1,0:T(8,128)(2,1)} %bitcast.5), custom_call_target="tpu_custom_call" | custom-call | tf_op jit(solution)/shard_map/expert_layer/pallas_call | solution.py:339
  183.9 1.9 %copy.7 = bf16[128,2048]{1,0:T(8,128)(2,1)} copy(bf16[128,2048]{1,0:T(8,128)(2,1)} %expert_layer.1) | data formatting | bytes 1048576

commit v4 on v3

--- a/solution.py
+++ b/solution.py
@@ -24,7 +24,7 @@
 
 def kernel(cols, cap, slots, tokens_ref, ids_ref, gates_ref, w_in_hbm, w_out_hbm, out_ref,
            w_in, w_out, tok0, tok1, tok2, blk0, blk1, blk2, recv, mid0, mid1, mid2, end0, end1, end2,
-           sum0, sum1, sum2, got0, got1, got2, ids_all, gates_all, places, cnt_mine, cnt_all, acc,
+           sum0, sum1, sum2, got0, got1, got2, ids_all, gates_all, places, scales, cnt_mine, cnt_all, acc,
            w_sem, ids_send, ids_recv, gate_send, gate_recv, cnt_send, cnt_recv, tok_send_a, tok_send_b, tok_recv,
            blk_send, blk_recv, mid_send, mid_recv, end_send, end_recv, sum_send, sum_recv):
     toks, blks = (tok0, tok1, tok2), (blk0, blk1, blk2)
@@ -61,9 +61,14 @@
     load_in = pltpu.make_async_copy(w_in_hbm, w_in, w_sem.at[0])
     load_out = pltpu.make_async_copy(w_out_hbm, w_out, w_sem.at[1])
 
-    for p in range(3):
-        for step in (1, 3):
-            send(tokens_ref.at[:, part(p)], toks[p].at[0, step], tok_send_a.at[p], tok_recv.at[p, step], device(0, {AXES[p][0]: step}))
+    def across(k):
+        return device(lax.div(k, 64), {Z: lax.rem(lax.div(k, 16), 4), Y: lax.rem(lax.div(k, 4), 4), X: lax.rem(k, 4)})
+
+    barrier = pltpu.get_barrier_semaphore()
+
+    @pl.loop(1, N)
+    def _(k):
+        pl.semaphore_signal(barrier, inc=1, device_id=across(k), device_id_type=MESH)
 
     mark = jnp.zeros((N, tok), F32)
     for j in range(top):
@@ -71,11 +76,28 @@
     counts = lax.dot_general(jnp.ones((8, tok), BF16), mark.astype(BF16), (((1,), (1,)), ((), ())), preferred_element_type=F32)
     cnt_mine[...] = counts[:1]
     cnt_all[pl.ds(me, 1)] = counts[:1][None]
+    for p in range(3):
+        toks[p][0, 0] = tokens_ref[:, part(p)]
+        ids_all[p, 0] = ids_ref[...]
+        gates_all[p, 0] = gates_ref[...]
+    load_in.start()
+    load_out.start()
+    pl.semaphore_wait(barrier, N - 1)
+
+    for p in range(3):
+        for step in (1, 3):
+            send(tokens_ref.at[:, part(p)], toks[p].at[0, step], tok_send_a.at[p], tok_recv.at[p, step], device(0, {AXES[p][0]: step}))
+
+    def gather_on(p, a, src):
+        for step in (1, 3):
+            send(src, toks[p].at[step, a], tok_send_b.at[p], tok_recv.at[p, 4 * step + a], device(0, {AXES[p][1]: step}))
+
+    for p in range(3):
+        gather_on(p, 0, tokens_ref.at[:, part(p)])
 
     @pl.loop(1, N)
     def _(k):
-        d = {Z: lax.rem(lax.div(k, 16), 4), Y: lax.rem(lax.div(k, 4), 4), X: lax.rem(k, 4)}
-        send(cnt_mine, cnt_all.at[me], cnt_send, cnt_recv, device(lax.div(k, 64), d))
+        send(cnt_mine, cnt_all.at[me], cnt_send, cnt_recv, across(k))
 
     for p in range(3):
         d1, d2, d3 = AXES[p]
@@ -88,23 +110,8 @@
         def _(i):
             send(gates_ref, gates_all.at[p, i], gate_send.at[p], gate_recv.at[p], device(0, {d1: i}))
 
-    def gather_on(p, a, src):
-        for step in (1, 3):
-            send(src, toks[p].at[step, a], tok_send_b.at[p], tok_recv.at[p, 4 * step + a], device(0, {AXES[p][1]: step}))
-
-    for p in range(3):
-        gather_on(p, 0, tokens_ref.at[:, part(p)])
-
-    load_in.start()
-    load_out.start()
-
     def arrived(p, b, a):
         wait_for(toks[p].at[b, a], tok_recv.at[p, 4 * b + a])
-
-    for p in range(3):
-        toks[p][0, 0] = tokens_ref[:, part(p)]
-        ids_all[p, 0] = ids_ref[...]
-        gates_all[p, 0] = gates_ref[...]
 
     half = tok // 2
     for p in range(3):
@@ -174,12 +181,12 @@
 
     for p in range(3):
         t = toks[p]
-        for step, pieces in ((1, (0, 1)), (3, (3, 2))):
+        for step, pieces in ((1, (0, 2)), (3, (1, 3))):
             for a in pieces:
                 arrived(p, step, a)
                 send(t.at[step, a], t.at[2, a], tok_send_b.at[p], tok_recv.at[p, 8 + a], device(0, {AXES[p][1]: step}))
 
-    for step, rest in ((1, (3, 2)), (3, (0, 1))):
+    for step, rest in ((1, (1, 3)), (3, (0, 2))):
         for p in range(3):
             for a in rest:
                 arrived(p, step, a)
@@ -252,18 +259,20 @@
                     send(mids[p].at[middle(p, first, s2)], ends[p].at[first, s2],
                          end_send.at[p], end_recv.at[p, high[d1]], device(0, {d2: 4 - s2}))
 
-    def combine(p, h):
+    def weigh(p):
         d1, d2, d3 = AXES[p]
         e = iota((32, tok), 0)
         expert_id = number((e >> 2) & 1, {d2: e >> 3, d3: e & 3})
-        scales = []
-        for s1 in (2 * h, 2 * h + 1):
+
+        @pl.loop(0, 4)
+        def _(s1):
+            ids, gts = ids_all[p, s1], gates_all[p, s1]
             mark = jnp.zeros((32, tok), F32)
             gate = jnp.zeros((32, tok), F32)
             for j in range(top):
-                hit = ids_all[p, s1, j:j + 1, :] == expert_id
+                hit = ids[j:j + 1, :] == expert_id
                 mark = jnp.where(hit, 1.0, mark)
-                gate = jnp.where(hit, gates_all[p, s1, j:j + 1, :], gate)
+                gate = jnp.where(hit, gts[j:j + 1, :], gate)
             place = jnp.dot(mark.astype(BF16), later, preferred_element_type=F32)
             place = jnp.where(mark > 0, place, -1.0)
             scale = jnp.where(place[:, None, :] == iota((32, slots, tok), 1).astype(F32), gate[:, None, :], 0.0)
@@ -272,17 +281,19 @@
             left = scale - high.astype(F32)
             mid = left.astype(BF16)
             low = (left - mid.astype(F32)).astype(BF16)
-            scales.append(jnp.concatenate([high, mid, low], axis=0))
+            scales[4 * p + s1] = jnp.concatenate([high, mid, low], axis=0)
+
+    def combine(p, h):
         wait_for(ends[p].at[pl.ds(2 * h, 2), pl.ds(1, 3)], end_recv.at[p, h])
-        for s1 in (2 * h, 2 * h + 1):
+        for s1 in (2 * h + 1, 2 * h):
             rows = ends[p][s1].reshape(32 * slots, cols[p][1])
-            mixed = jnp.dot(scales[s1 - 2 * h], rows, preferred_element_type=F32)
+            mixed = jnp.dot(scales[4 * p + s1], rows, preferred_element_type=F32)
             mixed = mixed[:tok] + (mixed[tok:2 * tok] + mixed[2 * tok:])
             if s1 == 0:
                 acc[:, part(p)] = tokens_ref[:, part(p)].astype(F32) + mixed
             else:
                 sums[p][s1 - 1] = mixed
-                send(sums[p].at[s1 - 1], gots[p].at[s1 - 1], sum_send.at[p], sum_recv.at[p, s1 - 1], device(0, {d1: 4 - s1}))
+                send(sums[p].at[s1 - 1], gots[p].at[s1 - 1], sum_send.at[p], sum_recv.at[p, s1 - 1], device(0, {AXES[p][0]: 4 - s1}))
 
     pl.loop(0, 1)(expert)
 
@@ -297,9 +308,14 @@
     @pl.loop(1, 8)
     def _(j):
         expert(j)
-        pass_on(j - 1)
-
-    pl.loop(7, 8)(pass_on)
+
+        @pl.when(j > 3)
+        def _():
+            pass_on(j - 3)
+
+    pl.loop(5, 8)(pass_on)
+    for p in range(3):
+        weigh(p)
     for h in range(2):
         for p in range(3):
             combine(p, h)
@@ -354,13 +370,14 @@
                 pltpu.VMEM((3, 16, top, tok), I32),
                 pltpu.VMEM((3, 4, top, tok), F32),
                 pltpu.VMEM((3, 128, tok), F32),
+                pltpu.VMEM((12, 3 * tok, 32 * slots), BF16),
                 pltpu.VMEM((1, N), F32),
                 pltpu.VMEM((N, 1, N), F32),
                 pltpu.VMEM((tok, width), F32),
                 dma((2,)), dma((3,)), dma((3,)), dma((3,)), dma((3,)), dma, dma, dma((3,)), dma((3,)), dma((3, 16)),
                 dma((3,)), dma((3, 8)), dma((3,)), dma((3, 8)), dma((3,)), dma((3, 2)), dma((3,)), dma((3, 3)),
             ],
-            compiler_params=pltpu.CompilerParams(has_side_effects=True, vmem_limit_bytes=67043328),
+            compiler_params=pltpu.CompilerParams(collective_id=0, has_side_effects=True, vmem_limit_bytes=67043328),
             name='expert_layer',
         )(tokens, expert_ids.T, gate_weights.T, w_in.reshape(width, ff), w_out.reshape(ff, width))
 

time: 186 us -> 171 us (0.919)
  Pallas kernels: 184 us -> 169 us
    pallas_call x1, Pallas kernels: 184 us -> 169 us  [device_fn(): pl.pallas_call(functools.partial(kernel, cols, cap, slots), out_shape=jax...]
where the time goes in v4:
time: 171 us
  Pallas kernels  169 us (99%)
  local copies, waits for them, and re-layouts  1.88 us (1%)
    pallas_call x1, Pallas kernels, device_fn(): pl.pallas_call(functools.partial(kernel, cols, cap, slots), out_shape=jax...  169 us

profile of v4, /device:TPU:1, one launch (start us, length us, event | category | flops | bytes accessed | tf_op | source)
XLA Modules:
  0.0 171.0 jit_solution(13097740329461550411)
XLA Ops:
  0.0 169.1 %expert_layer.1 = bf16[128,2048]{1,0:T(8,128)(2,1)} custom-call(bf16[128,2048]{1,0:T(8,128)(2,1)} %tokens_ref.1, s32[8,128]{1,0:T(8,128)} %bitcast.6, f32[8,128]{1,0:T(8,128)} %bitcast.7, bf16[2048,768]{1,0:T(8,128)(2,1)} %bitcast.4, bf16[768,2048]{1,0:T(8,128)(2,1)} %bitcast.5), custom_call_target="tpu_custom_call" | custom-call | tf_op jit(solution)/shard_map/expert_layer/pallas_call | solution.py:355
  169.2 1.9 %copy.7 = bf16[128,2048]{1,0:T(8,128)(2,1)} copy(bf16[128,2048]{1,0:T(8,128)(2,1)} %expert_layer.1) | data formatting | bytes 1048576

commit v5 on v4

--- a/solution.py
+++ b/solution.py
@@ -218,6 +218,9 @@
         o = jnp.dot(hidden, w_out[...], preferred_element_type=F32).astype(BF16)
         recv[cube] = o.reshape(2, 2, 2, 2, slots, width)
 
+    def hand_out(j):
+        high = halves(j)
+        pair = [pl.ds(2 * h, 2) for h in high]
         for p in range(3):
             d3 = AXES[p][2]
             rest = [pair[a] for a in range(3) if a != d3]
@@ -244,10 +247,10 @@
         for p in range(3):
             d1, d2, d3 = AXES[p]
 
-            @pl.when(high[d3] == 1)
+            @pl.when(high[d3] == 0)
             def _():
-                wait_blocks(p, 0, blks[p], mid_recv.at[p, j - (4, 2, 1)[d3]])
-                wait_blocks(p, 1, blks[p], mid_recv.at[p, j])
+                wait_blocks(p, 1, blks[p], mid_recv.at[p, j + (4, 2, 1)[d3]])
+                wait_blocks(p, 0, blks[p], mid_recv.at[p, j])
                 first = pl.ds(2 * high[d1], 2)
 
                 @pl.when(high[d2] == 0)
@@ -305,18 +308,24 @@
     for p in range(3):
         wait_for(gates_all.at[p, pl.ds(1, 3)], gate_recv.at[p])
 
-    @pl.loop(1, 8)
-    def _(j):
-        expert(j)
-
-        @pl.when(j > 3)
+    @pl.loop(0, 7)
+    def _(i):
+        expert(7 - i)
+        hand_out(7 - i)
+
+        @pl.when(i > 2)
         def _():
-            pass_on(j - 3)
-
-    pl.loop(5, 8)(pass_on)
+            pass_on(10 - i)
+
+    pl.loop(0, 1)(hand_out)
+
+    @pl.loop(0, 4)
+    def _(i):
+        pass_on(3 - i)
+
     for p in range(3):
         weigh(p)
-    for h in range(2):
+    for h in (1, 0):
         for p in range(3):
             combine(p, h)
 

time: 171 us -> 168 us (0.982)
  Pallas kernels: 169 us -> 166 us
    pallas_call x1, Pallas kernels: 169 us -> 166 us  [device_fn(): pl.pallas_call(functools.partial(kernel, cols, cap, slots), out_shape=jax...]
where the time goes in v5:
time: 168 us
  Pallas kernels  166 us (99%)
  local copies, waits for them, and re-layouts  1.88 us (1%)
    pallas_call x1, Pallas kernels, device_fn(): pl.pallas_call(functools.partial(kernel, cols, cap, slots), out_shape=jax...  166 us

profile of v5, /device:TPU:1, one launch (start us, length us, event | category | flops | bytes accessed | tf_op | source)
XLA Modules:
  0.0 167.7 jit_solution(17387437754097212494)
XLA Ops:
  0.0 165.8 %expert_layer.1 = bf16[128,2048]{1,0:T(8,128)(2,1)} custom-call(bf16[128,2048]{1,0:T(8,128)(2,1)} %tokens_ref.1, s32[8,128]{1,0:T(8,128)} %bitcast.6, f32[8,128]{1,0:T(8,128)} %bitcast.7, bf16[2048,768]{1,0:T(8,128)(2,1)} %bitcast.4, bf16[768,2048]{1,0:T(8,128)(2,1)} %bitcast.5), custom_call_target="tpu_custom_call" | custom-call | tf_op jit(solution)/shard_map/expert_layer/pallas_call | solution.py:364
  165.8 1.9 %copy.7 = bf16[128,2048]{1,0:T(8,128)(2,1)} copy(bf16[128,2048]{1,0:T(8,128)(2,1)} %expert_layer.1) | data formatting | bytes 1048576

commit v6 on v5

--- a/solution.py
+++ b/solution.py
@@ -24,8 +24,8 @@
 
 def kernel(cols, cap, slots, tokens_ref, ids_ref, gates_ref, w_in_hbm, w_out_hbm, out_ref,
            w_in, w_out, tok0, tok1, tok2, blk0, blk1, blk2, recv, mid0, mid1, mid2, end0, end1, end2,
-           sum0, sum1, sum2, got0, got1, got2, ids_all, gates_all, places, scales, cnt_mine, cnt_all, acc,
-           w_sem, ids_send, ids_recv, gate_send, gate_recv, cnt_send, cnt_recv, tok_send_a, tok_send_b, tok_recv,
+           sum0, sum1, sum2, got0, got1, got2, info, info_all, places, scales, cnt_out, cnt_in, cnt_row, acc,
+           w_sem, info_send_a, info_send_b, info_recv, cnt_send, cnt_recv, line_sem, tok_send_a, tok_send_b, tok_recv,
            blk_send, blk_recv, mid_send, mid_recv, end_send, end_recv, sum_send, sum_recv):
     toks, blks = (tok0, tok1, tok2), (blk0, blk1, blk2)
     mids, ends = (mid0, mid1, mid2), (end0, end1, end2)
@@ -61,56 +61,39 @@
     load_in = pltpu.make_async_copy(w_in_hbm, w_in, w_sem.at[0])
     load_out = pltpu.make_async_copy(w_out_hbm, w_out, w_sem.at[1])
 
-    def across(k):
-        return device(lax.div(k, 64), {Z: lax.rem(lax.div(k, 16), 4), Y: lax.rem(lax.div(k, 4), 4), X: lax.rem(k, 4)})
-
+    near = [device(0, {a: step}) for a in range(3) for step in (1, 3)] + [device(1, {})]
     barrier = pltpu.get_barrier_semaphore()
-
-    @pl.loop(1, N)
-    def _(k):
-        pl.semaphore_signal(barrier, inc=1, device_id=across(k), device_id_type=MESH)
-
-    mark = jnp.zeros((N, tok), F32)
-    for j in range(top):
-        mark = jnp.where(ids_ref[j:j + 1, :] == iota((N, tok), 0), 1.0, mark)
-    counts = lax.dot_general(jnp.ones((8, tok), BF16), mark.astype(BF16), (((1,), (1,)), ((), ())), preferred_element_type=F32)
-    cnt_mine[...] = counts[:1]
-    cnt_all[pl.ds(me, 1)] = counts[:1][None]
-    for p in range(3):
-        toks[p][0, 0] = tokens_ref[:, part(p)]
-        ids_all[p, 0] = ids_ref[...]
-        gates_all[p, 0] = gates_ref[...]
+    for to in near:
+        pl.semaphore_signal(barrier, inc=1, device_id=to, device_id_type=MESH)
     load_in.start()
     load_out.start()
-    pl.semaphore_wait(barrier, N - 1)
+    info[:top] = ids_ref[...].astype(F32)
+    info[top:] = gates_ref[...]
+    pl.semaphore_wait(barrier, len(near))
 
     for p in range(3):
         for step in (1, 3):
-            send(tokens_ref.at[:, part(p)], toks[p].at[0, step], tok_send_a.at[p], tok_recv.at[p, step], device(0, {AXES[p][0]: step}))
-
-    def gather_on(p, a, src):
+            to = device(0, {AXES[p][0]: step})
+            send(info, info_all.at[p, step], info_send_a.at[p], info_recv.at[p, step], to)
+            send(tokens_ref.at[:, part(p)], toks[p].at[0, step], tok_send_a.at[p], tok_recv.at[p, step], to)
+
+    ids = pl.ds(0, top)
+
+    def gather_on(p, a, src, ids_src):
         for step in (1, 3):
-            send(src, toks[p].at[step, a], tok_send_b.at[p], tok_recv.at[p, 4 * step + a], device(0, {AXES[p][1]: step}))
-
-    for p in range(3):
-        gather_on(p, 0, tokens_ref.at[:, part(p)])
-
-    @pl.loop(1, N)
-    def _(k):
-        send(cnt_mine, cnt_all.at[me], cnt_send, cnt_recv, across(k))
-
-    for p in range(3):
-        d1, d2, d3 = AXES[p]
-
-        @pl.loop(1, 16)
-        def _(i):
-            send(ids_ref, ids_all.at[p, i], ids_send.at[p], ids_recv.at[p], device(0, {d2: lax.div(i, 4), d1: lax.rem(i, 4)}))
-
-        @pl.loop(1, 4)
-        def _(i):
-            send(gates_ref, gates_all.at[p, i], gate_send.at[p], gate_recv.at[p], device(0, {d1: i}))
+            to = device(0, {AXES[p][1]: step})
+            send(ids_src, info_all.at[p, 4 * step + a, ids], info_send_b.at[p], info_recv.at[p, 4 * step + a], to)
+            send(src, toks[p].at[step, a], tok_send_b.at[p], tok_recv.at[p, 4 * step + a], to)
+
+    for p in range(3):
+        gather_on(p, 0, tokens_ref.at[:, part(p)], info.at[ids])
+    for p in range(3):
+        toks[p][0, 0] = tokens_ref[:, part(p)]
+        info_all[p, 0] = info[...]
 
     def arrived(p, b, a):
+        what = info_all.at[p, a] if b == 0 else info_all.at[p, 4 * b + a, ids]
+        wait_for(what, info_recv.at[p, 4 * b + a])
         wait_for(toks[p].at[b, a], tok_recv.at[p, 4 * b + a])
 
     half = tok // 2
@@ -118,35 +101,20 @@
         t = toks[p]
         for step, rows in ((1, pl.ds(0, half)), (3, pl.ds(half, half))):
             arrived(p, 0, step)
-            send(t.at[0, step, rows], t.at[0, 2, rows], tok_send_a.at[p], tok_recv.at[p, 2], device(0, {AXES[p][0]: step}))
-            gather_on(p, step, t.at[0, step])
-
-    wait_for(cnt_all.at[pl.ds(0, N - 1)], cnt_recv)
-    below = (iota((N, N), 1) < iota((N, N), 0)).astype(BF16)
-    before = jnp.dot(below, jnp.sum(cnt_all[...], axis=1).astype(BF16), preferred_element_type=F32)
-    room = jnp.clip(cap - before, 0.0, float(slots)).astype(BF16)
+            to = device(0, {AXES[p][0]: step})
+            if step == 1:
+                send(info_all.at[p, 1], info_all.at[p, 2], info_send_a.at[p], info_recv.at[p, 2], to)
+            send(t.at[0, step, rows], t.at[0, 2, rows], tok_send_a.at[p], tok_recv.at[p, 2], to)
+            gather_on(p, step, t.at[0, step], info_all.at[p, step, ids])
+
+    for p in range(3):
+        arrived(p, 0, 2)
+        gather_on(p, 2, toks[p].at[0, 2], info_all.at[p, 2, ids])
+
+    pl.semaphore_signal(line_sem, inc=1, device_id=near[6], device_id_type=MESH)
+    pl.semaphore_wait(line_sem, 1)
 
     later = (iota((tok, tok), 0) < iota((tok, tok), 1)).astype(BF16)
-    for p in range(3):
-        d1, d2, d3 = AXES[p]
-        wait_for(ids_all.at[p, pl.ds(1, 15)], ids_recv.at[p])
-        dest = iota((8, tok), 0)
-        expert_id = number(dest >> 2, {d3: dest & 3})[None]
-        mark = jnp.zeros((16, 8, tok), F32)
-        for j in range(top):
-            mark = jnp.where(ids_all[p, :, j:j + 1, :] == expert_id, 1.0, mark)
-        mark = mark.reshape(128, tok)
-        place = jnp.dot(mark.astype(BF16), later, preferred_element_type=F32)
-        i = iota((128, N), 0)
-        source = number(0, {d2: 4 - (i >> 5), d1: 4 - ((i >> 3) & 3)})
-        mine = jnp.dot((source == iota((128, N), 1)).astype(BF16), room, preferred_element_type=F32)
-        target = number((i >> 2) & 1, {d3: i & 3})
-        mine = jnp.sum(jnp.where(target == iota((128, N), 1), mine, 0.0), axis=1, keepdims=True)
-        places[p] = jnp.where((mark > 0) & (place < mine), place, -1.0)
-
-    for p in range(3):
-        arrived(p, 0, 2)
-        gather_on(p, 2, toks[p].at[0, 2])
 
     def where_in(p, d_core, s1, s2, s3):
         at = [None] * 3
@@ -156,10 +124,29 @@
 
     def build(p, b):
         t, blk = toks[p], blks[p]
+        d3 = AXES[p][2]
+        dest = iota((8, tok), 0)
+        expert_id = number(dest >> 2, {d3: dest & 3}).astype(F32)[None]
+        mark = jnp.zeros((4, 8, tok), F32)
+        for j in range(top):
+            mark = jnp.where(info_all[p, pl.ds(4 * b, 4), j:j + 1, :] == expert_id, 1.0, mark)
+        mark = mark.reshape(32, tok)
+        place = jnp.dot(mark.astype(BF16), later, preferred_element_type=F32)
+        places[...] = jnp.where(mark > 0, place, -1.0)
+        if p == 0:
+            wide = [jnp.zeros((32, tok), F32)] * 4
+            wide[b] = mark
+            wide = jnp.concatenate(wide, axis=0).astype(BF16)
+            cnt_out[b] = lax.dot_general(jnp.ones((8, tok), BF16), wide, (((1,), (1,)), ((), ())), preferred_element_type=F32)
+            cnt_in[0, b] = cnt_out[b]
+
+            @pl.loop(1, 8)
+            def _(d):
+                send(cnt_out.at[b], cnt_in.at[d, b], cnt_send, cnt_recv, device(lax.div(d, 4), {d3: lax.rem(d, 4)}))
 
         @pl.loop(0, 4)
         def _(a):
-            place = places[p, pl.ds((4 * b + a) * 8, 8), :]
+            place = places[pl.ds(a * 8, 8), :]
             pick = place[:, None, :] == iota((8, slots, tok), 1).astype(F32)
             pick = jnp.where(pick, 1.0, 0.0).reshape(8 * slots, tok).astype(BF16)
             rows = jnp.dot(pick, t[b, a], preferred_element_type=F32).astype(BF16).reshape(8, slots, cols[p][1])
@@ -184,7 +171,9 @@
         for step, pieces in ((1, (0, 2)), (3, (1, 3))):
             for a in pieces:
                 arrived(p, step, a)
-                send(t.at[step, a], t.at[2, a], tok_send_b.at[p], tok_recv.at[p, 8 + a], device(0, {AXES[p][1]: step}))
+                to = device(0, {AXES[p][1]: step})
+                send(info_all.at[p, 4 * step + a, ids], info_all.at[p, 8 + a, ids], info_send_b.at[p], info_recv.at[p, 8 + a], to)
+                send(t.at[step, a], t.at[2, a], tok_send_b.at[p], tok_recv.at[p, 8 + a], to)
 
     for step, rest in ((1, (1, 3)), (3, (0, 2))):
         for p in range(3):
@@ -218,6 +207,21 @@
         o = jnp.dot(hidden, w_out[...], preferred_element_type=F32).astype(BF16)
         recv[cube] = o.reshape(2, 2, 2, 2, slots, width)
 
+    def drop(j):
+        high = halves(j)
+        cube = (slice(None), *[pl.ds(2 * h, 2) for h in high])
+        rows = 16 * slots
+        r = iota((rows, N), 0)
+        i = r // slots
+        taker = number((i >> 3) & 1, {Z: 4 - (2 * high[Z] + ((i >> 2) & 1)), Y: 4 - (2 * high[Y] + ((i >> 1) & 1)), X: 4 - (2 * high[X] + (i & 1))})
+        c = iota((rows, N), 1)
+        d1, d2, d3 = AXES[0]
+        source = number((c >> 2) & 1, {d1: 4 - ((c >> 3) & 3), d2: 4 - (c >> 5), d3: 4 - (c & 3)})
+        before = jnp.sum(jnp.where(source < taker, cnt_row[...], 0.0), axis=1, keepdims=True)
+        keep = before + (iota((rows, 1), 0) % slots).astype(F32) < float(cap)
+        o = recv[cube].reshape(rows, width)
+        recv[cube] = jnp.where(keep, o, jnp.zeros_like(o)).reshape(2, 2, 2, 2, slots, width)
+
     def hand_out(j):
         high = halves(j)
         pair = [pl.ds(2 * h, 2) for h in high]
@@ -265,11 +269,11 @@
     def weigh(p):
         d1, d2, d3 = AXES[p]
         e = iota((32, tok), 0)
-        expert_id = number((e >> 2) & 1, {d2: e >> 3, d3: e & 3})
+        expert_id = number((e >> 2) & 1, {d2: e >> 3, d3: e & 3}).astype(F32)
 
         @pl.loop(0, 4)
         def _(s1):
-            ids, gts = ids_all[p, s1], gates_all[p, s1]
+            ids, gts = info_all[p, s1, :top], info_all[p, s1, top:]
             mark = jnp.zeros((32, tok), F32)
             gate = jnp.zeros((32, tok), F32)
             for j in range(top):
@@ -305,18 +309,24 @@
             arrived(p, 2, a)
         build(p, 2)
 
-    for p in range(3):
-        wait_for(gates_all.at[p, pl.ds(1, 3)], gate_recv.at[p])
+    wait_for(cnt_in.at[pl.ds(1, 7)], cnt_recv)
+    row = jnp.zeros((1, N), F32)
+    for d in range(8):
+        both = sum(cnt_in[d, b][:1] for b in range(4))
+        row = row + jnp.where(iota((1, N), 1) % 8 == d, both, 0.0)
+    cnt_row[...] = row
 
     @pl.loop(0, 7)
     def _(i):
         expert(7 - i)
+        drop(7 - i)
         hand_out(7 - i)
 
         @pl.when(i > 2)
         def _():
             pass_on(10 - i)
 
+    pl.loop(0, 1)(drop)
     pl.loop(0, 1)(hand_out)
 
     @pl.loop(0, 4)
@@ -336,10 +346,10 @@
             total = total + gots[p][i]
         out_ref[:, part(p)] = total.astype(BF16)
 
-    wait_for(cnt_all.at[pl.ds(0, N - 1)], cnt_send)
-    for p in range(3):
-        wait_for(ids_all.at[p, pl.ds(1, 15)], ids_send.at[p])
-        wait_for(gates_all.at[p, pl.ds(1, 3)], gate_send.at[p])
+    wait_for(cnt_in.at[pl.ds(1, 7)], cnt_send)
+    for p in range(3):
+        wait_for(info_all.at[p, pl.ds(0, 3)], info_send_a.at[p])
+        wait_for(info_all.at[p, pl.ds(0, 12), ids], info_send_b.at[p])
         wait_for(toks[p].at[0, pl.ds(0, 3)], tok_send_a.at[p])
         wait_for(toks[p].at[pl.ds(0, 3)], tok_send_b.at[p])
         wait_for(blks[p].at[:, pl.ds(1, 7)], blk_send.at[p])
@@ -376,14 +386,15 @@
                 *[pltpu.VMEM((4, 4, 8, slots, s), BF16) for s in sizes],
                 *[pltpu.VMEM((3, tok, s), F32) for s in sizes],
                 *[pltpu.VMEM((3, tok, s), F32) for s in sizes],
-                pltpu.VMEM((3, 16, top, tok), I32),
-                pltpu.VMEM((3, 4, top, tok), F32),
-                pltpu.VMEM((3, 128, tok), F32),
+                pltpu.VMEM((2 * top, tok), F32),
+                pltpu.VMEM((3, 16, 2 * top, tok), F32),
+                pltpu.VMEM((32, tok), F32),
                 pltpu.VMEM((12, 3 * tok, 32 * slots), BF16),
+                pltpu.VMEM((4, 8, N), F32),
+                pltpu.VMEM((8, 4, 8, N), F32),
                 pltpu.VMEM((1, N), F32),
-                pltpu.VMEM((N, 1, N), F32),
                 pltpu.VMEM((tok, width), F32),
-                dma((2,)), dma((3,)), dma((3,)), dma((3,)), dma((3,)), dma, dma, dma((3,)), dma((3,)), dma((3, 16)),
+                dma((2,)), dma((3,)), dma((3,)), dma((3, 16)), dma, dma, pltpu.SemaphoreType.REGULAR, dma((3,)), dma((3,)), dma((3, 16)),
                 dma((3,)), dma((3, 8)), dma((3,)), dma((3, 8)), dma((3,)), dma((3, 2)), dma((3,)), dma((3, 3)),
             ],
             compiler_params=pltpu.CompilerParams(collective_id=0, has_side_effects=True, vmem_limit_bytes=67043328),

time: 168 us -> 163 us (0.970)
  Pallas kernels: 166 us -> 161 us
    pallas_call x1, Pallas kernels: 166 us -> 161 us  [device_fn(): pl.pallas_call(functools.partial(kernel, cols, cap, slots), out_shape=jax...]
where the time goes in v6:
time: 163 us
  Pallas kernels  161 us (99%)
  local copies, waits for them, and re-layouts  1.88 us (1%)
    pallas_call x1, Pallas kernels, device_fn(): pl.pallas_call(functools.partial(kernel, cols, cap, slots), out_shape=jax...  161 us

profile of v6, /device:TPU:1, one launch (start us, length us, event | category | flops | bytes accessed | tf_op | source)
XLA Modules:
  0.0 162.8 jit_solution(14645315381096266675)
XLA Ops:
  0.0 160.9 %expert_layer.1 = bf16[128,2048]{1,0:T(8,128)(2,1)} custom-call(bf16[128,2048]{1,0:T(8,128)(2,1)} %tokens_ref.1, s32[8,128]{1,0:T(8,128)} %bitcast.6, f32[8,128]{1,0:T(8,128)} %bitcast.7, bf16[2048,768]{1,0:T(8,128)(2,1)} %bitcast.4, bf16[768,2048]{1,0:T(8,128)(2,1)} %bitcast.5), custom_call_target="tpu_custom_call" | custom-call | tf_op jit(solution)/shard_map/expert_layer/pallas_call | solution.py:374
  160.9 1.9 %copy.7 = bf16[128,2048]{1,0:T(8,128)(2,1)} copy(bf16[128,2048]{1,0:T(8,128)(2,1)} %expert_layer.1) | data formatting | bytes 1048576

commit v7 on v6

--- a/solution.py
+++ b/solution.py
@@ -163,17 +163,19 @@
                      recv.at[where_in(p, d_core, pl.ds(2 * h, 2), b, s3) + (slice(None), part(p))],
                      blk_send.at[p], blk_recv.at[p, cube], device(d_core, {AXES[p][2]: s3}))
 
+    def relay(p, step, a):
+        t, to = toks[p], device(0, {AXES[p][1]: step})
+        arrived(p, step, a)
+        send(info_all.at[p, 4 * step + a, ids], info_all.at[p, 8 + a, ids], info_send_b.at[p], info_recv.at[p, 8 + a], to)
+        send(t.at[step, a], t.at[2, a], tok_send_b.at[p], tok_recv.at[p, 8 + a], to)
+
+    for p in range(3):
+        relay(p, 1, 0)
     for p in range(3):
         build(p, 0)
 
-    for p in range(3):
-        t = toks[p]
-        for step, pieces in ((1, (0, 2)), (3, (1, 3))):
-            for a in pieces:
-                arrived(p, step, a)
-                to = device(0, {AXES[p][1]: step})
-                send(info_all.at[p, 4 * step + a, ids], info_all.at[p, 8 + a, ids], info_send_b.at[p], info_recv.at[p, 8 + a], to)
-                send(t.at[step, a], t.at[2, a], tok_send_b.at[p], tok_recv.at[p, 8 + a], to)
+    for p, step, a in [(p, step, a) for step, a in ((3, 1), (3, 3), (1, 2)) for p in range(3)]:
+        relay(p, step, a)
 
     for step, rest in ((1, (1, 3)), (3, (0, 2))):
         for p in range(3):
@@ -290,17 +292,15 @@
             low = (left - mid.astype(F32)).astype(BF16)
             scales[4 * p + s1] = jnp.concatenate([high, mid, low], axis=0)
 
-    def combine(p, h):
-        wait_for(ends[p].at[pl.ds(2 * h, 2), pl.ds(1, 3)], end_recv.at[p, h])
-        for s1 in (2 * h + 1, 2 * h):
-            rows = ends[p][s1].reshape(32 * slots, cols[p][1])
-            mixed = jnp.dot(scales[4 * p + s1], rows, preferred_element_type=F32)
-            mixed = mixed[:tok] + (mixed[tok:2 * tok] + mixed[2 * tok:])
-            if s1 == 0:
-                acc[:, part(p)] = tokens_ref[:, part(p)].astype(F32) + mixed
-            else:
-                sums[p][s1 - 1] = mixed
-                send(sums[p].at[s1 - 1], gots[p].at[s1 - 1], sum_send.at[p], sum_recv.at[p, s1 - 1], device(0, {AXES[p][0]: 4 - s1}))
+    def combine(p, s1):
+        rows = ends[p][s1].reshape(32 * slots, cols[p][1])
+        mixed = jnp.dot(scales[4 * p + s1], rows, preferred_element_type=F32)
+        mixed = mixed[:tok] + (mixed[tok:2 * tok] + mixed[2 * tok:])
+        if s1 == 0:
+            acc[:, part(p)] = tokens_ref[:, part(p)].astype(F32) + mixed
+        else:
+            sums[p][s1 - 1] = mixed
+            send(sums[p].at[s1 - 1], gots[p].at[s1 - 1], sum_send.at[p], sum_recv.at[p, s1 - 1], device(0, {AXES[p][0]: 4 - s1}))
 
     pl.loop(0, 1)(expert)
 
@@ -315,6 +315,8 @@
         both = sum(cnt_in[d, b][:1] for b in range(4))
         row = row + jnp.where(iota((1, N), 1) % 8 == d, both, 0.0)
     cnt_row[...] = row
+    pl.loop(0, 1)(drop)
+    pl.loop(0, 1)(hand_out)
 
     @pl.loop(0, 7)
     def _(i):
@@ -326,18 +328,21 @@
         def _():
             pass_on(10 - i)
 
-    pl.loop(0, 1)(drop)
-    pl.loop(0, 1)(hand_out)
-
     @pl.loop(0, 4)
     def _(i):
         pass_on(3 - i)
 
     for p in range(3):
         weigh(p)
-    for h in (1, 0):
-        for p in range(3):
-            combine(p, h)
+    for p in range(3):
+        wait_for(ends[p].at[pl.ds(2, 2), pl.ds(1, 3)], end_recv.at[p, 1])
+        combine(p, 2)
+        combine(p, 3)
+    for p in range(3):
+        wait_for(ends[p].at[pl.ds(0, 2), pl.ds(1, 3)], end_recv.at[p, 0])
+        combine(p, 1)
+    for p in range(3):
+        combine(p, 0)
 
     for p in range(3):
         total = acc[:, part(p)]

time: 163 us -> 162 us (level)
  no operation moved by 1% of the time
where the time goes in v7:
time: 162 us
  Pallas kernels  160 us (99%)
  local copies, waits for them, and re-layouts  1.88 us (1%)
    pallas_call x1, Pallas kernels, device_fn(): pl.pallas_call(functools.partial(kernel, cols, cap, slots), out_shape=jax...  160 us

profile of v7, /device:TPU:1, one launch (start us, length us, event | category | flops | bytes accessed | tf_op | source)
XLA Modules:
  0.0 162.3 jit_solution(5528444215974059078)
XLA Ops:
  0.0 160.4 %expert_layer.1 = bf16[128,2048]{1,0:T(8,128)(2,1)} custom-call(bf16[128,2048]{1,0:T(8,128)(2,1)} %tokens_ref.1, s32[8,128]{1,0:T(8,128)} %bitcast.6, f32[8,128]{1,0:T(8,128)} %bitcast.7, bf16[2048,768]{1,0:T(8,128)(2,1)} %bitcast.4, bf16[768,2048]{1,0:T(8,128)(2,1)} %bitcast.5), custom_call_target="tpu_custom_call" | custom-call | tf_op jit(solution)/shard_map/expert_layer/pallas_call | solution.py:379
  160.4 1.9 %copy.7 = bf16[128,2048]{1,0:T(8,128)(2,1)} copy(bf16[128,2048]{1,0:T(8,128)(2,1)} %expert_layer.1) | data formatting | bytes 1048576

commit v8 on v7

--- a/solution.py
+++ b/solution.py
@@ -153,15 +153,17 @@
             blk[b, :, a] = rows
             recv[where_in(p, 0, a, b, 0) + (slice(None), part(p))] = rows[0]
 
+    def post(b):
         for h in range(2):
             @pl.loop(1, 8)
             def _(d):
                 d_core, s3 = lax.div(d, 4), lax.rem(d, 4)
-                high = {AXES[p][0]: h, AXES[p][1]: b // 2, AXES[p][2]: lax.div(s3, 2)}
-                cube = high[Z] * 4 + high[Y] * 2 + high[X]
-                send(blk.at[b, d, pl.ds(2 * h, 2)],
-                     recv.at[where_in(p, d_core, pl.ds(2 * h, 2), b, s3) + (slice(None), part(p))],
-                     blk_send.at[p], blk_recv.at[p, cube], device(d_core, {AXES[p][2]: s3}))
+                for p in range(3):
+                    high = {AXES[p][0]: h, AXES[p][1]: b // 2, AXES[p][2]: lax.div(s3, 2)}
+                    cube = high[Z] * 4 + high[Y] * 2 + high[X]
+                    send(blks[p].at[b, d, pl.ds(2 * h, 2)],
+                         recv.at[where_in(p, d_core, pl.ds(2 * h, 2), b, s3) + (slice(None), part(p))],
+                         blk_send.at[p], blk_recv.at[p, cube], device(d_core, {AXES[p][2]: s3}))
 
     def relay(p, step, a):
         t, to = toks[p], device(0, {AXES[p][1]: step})
@@ -173,6 +175,7 @@
         relay(p, 1, 0)
     for p in range(3):
         build(p, 0)
+    post(0)
 
     for p, step, a in [(p, step, a) for step, a in ((3, 1), (3, 3), (1, 2)) for p in range(3)]:
         relay(p, step, a)
@@ -182,6 +185,7 @@
             for a in rest:
                 arrived(p, step, a)
             build(p, step)
+        post(step)
 
     load_in.wait()
     load_out.wait()
@@ -238,11 +242,19 @@
             def _():
                 mids[p][(*rest, 0)] = recv[(0, *along(0), slice(None), part(p))]
 
-            @pl.loop(jnp.where(high[d3] == 0, 1, 0), 4)
-            def _(i):
-                d_core, s3 = lax.div(i, 2), 2 * high[d3] + lax.rem(i, 2)
-                send(recv.at[(d_core, *along(s3), slice(None), part(p))], mids[p].at[(*rest, d_core * 4 + s3)],
-                     mid_send.at[p], mid_recv.at[p, j], device(d_core, {d3: 4 - s3}))
+        @pl.loop(0, 4)
+        def _(i):
+            d_core = lax.div(i, 2)
+            for p in range(3):
+                d3 = AXES[p][2]
+                s3 = 2 * high[d3] + lax.rem(i, 2)
+                rest = [pair[a] for a in range(3) if a != d3]
+                at = tuple(s3 if a == d3 else pair[a] for a in range(3))
+
+                @pl.when(i + high[d3] > 0)
+                def _():
+                    send(recv.at[(d_core, *at, slice(None), part(p))], mids[p].at[(*rest, d_core * 4 + s3)],
+                         mid_send.at[p], mid_recv.at[p, j], device(d_core, {d3: 4 - s3}))
 
     def middle(p, s1, s2):
         d1, d2 = AXES[p][:2]
@@ -308,6 +320,7 @@
         for a in range(4):
             arrived(p, 2, a)
         build(p, 2)
+    post(2)
 
     wait_for(cnt_in.at[pl.ds(1, 7)], cnt_recv)
     row = jnp.zeros((1, N), F32)

time: 162 us -> 163 us (level)
  no operation moved by 1% of the time
where the time goes in v8:
time: 163 us; the launch traced here: 162 us
  Pallas kernels  160 us (98%)
  local copies, waits for them, and re-layouts  1.88 us (1%)
    pallas_call x1, Pallas kernels, device_fn(): pl.pallas_call(functools.partial(kernel, cols, cap, slots), out_shape=jax...  160 us

profile of v8, /device:TPU:1, one launch (start us, length us, event | category | flops | bytes accessed | tf_op | source)
XLA Modules:
  0.0 162.2 jit_solution(13442524740258823034)
XLA Ops:
  0.0 160.3 %expert_layer.1 = bf16[128,2048]{1,0:T(8,128)(2,1)} custom-call(bf16[128,2048]{1,0:T(8,128)(2,1)} %tokens_ref.1, s32[8,128]{1,0:T(8,128)} %bitcast.6, f32[8,128]{1,0:T(8,128)} %bitcast.7, bf16[2048,768]{1,0:T(8,128)(2,1)} %bitcast.4, bf16[768,2048]{1,0:T(8,128)(2,1)} %bitcast.5), custom_call_target="tpu_custom_call" | custom-call | tf_op jit(solution)/shard_map/expert_layer/pallas_call | solution.py:392
  160.3 1.9 %copy.7 = bf16[128,2048]{1,0:T(8,128)(2,1)} copy(bf16[128,2048]{1,0:T(8,128)(2,1)} %expert_layer.1) | data formatting | bytes 1048576

commit v9 on v7

--- a/solution.py
+++ b/solution.py
@@ -248,6 +248,9 @@
         d1, d2 = AXES[p][:2]
         return (s1, s2) if d1 < d2 else (s2, s1)
 
+    def second(p, s1, s2, sem):
+        send(mids[p].at[middle(p, s1, s2)], ends[p].at[s1, s2], end_send.at[p], end_recv.at[p, sem], device(0, {AXES[p][1]: 4 - s2}))
+
     def pass_on(j):
         high = halves(j)
         for p in range(3):
@@ -265,8 +268,13 @@
 
                 @pl.loop(jnp.where(high[d2] == 0, 1, 2 * high[d2]), 2 * high[d2] + 2)
                 def _(s2):
-                    send(mids[p].at[middle(p, first, s2)], ends[p].at[first, s2],
-                         end_send.at[p], end_recv.at[p, high[d1]], device(0, {d2: 4 - s2}))
+                    @pl.when(high[d1] == 1)
+                    def _():
+                        second(p, pl.ds(2, 2), s2, 2)
+
+                    @pl.when(high[d1] == 0)
+                    def _():
+                        second(p, pl.ds(1, 1), s2, 1)
 
     def weigh(p):
         d1, d2, d3 = AXES[p]
@@ -332,16 +340,21 @@
     def _(i):
         pass_on(3 - i)
 
+    for s2 in (1, 3, 2):
+        for p in range(3):
+            second(p, pl.ds(0, 1), s2, 0)
+
     for p in range(3):
         weigh(p)
     for p in range(3):
-        wait_for(ends[p].at[pl.ds(2, 2), pl.ds(1, 3)], end_recv.at[p, 1])
+        wait_for(ends[p].at[pl.ds(2, 2), pl.ds(1, 3)], end_recv.at[p, 2])
         combine(p, 2)
         combine(p, 3)
     for p in range(3):
-        wait_for(ends[p].at[pl.ds(0, 2), pl.ds(1, 3)], end_recv.at[p, 0])
+        wait_for(ends[p].at[pl.ds(1, 1), pl.ds(1, 3)], end_recv.at[p, 1])
         combine(p, 1)
     for p in range(3):
+        wait_for(ends[p].at[pl.ds(0, 1), pl.ds(1, 3)], end_recv.at[p, 0])
         combine(p, 0)
 
     for p in range(3):
@@ -400,7 +413,7 @@
                 pltpu.VMEM((1, N), F32),
                 pltpu.VMEM((tok, width), F32),
                 dma((2,)), dma((3,)), dma((3,)), dma((3, 16)), dma, dma, pltpu.SemaphoreType.REGULAR, dma((3,)), dma((3,)), dma((3, 16)),
-                dma((3,)), dma((3, 8)), dma((3,)), dma((3, 8)), dma((3,)), dma((3, 2)), dma((3,)), dma((3, 3)),
+                dma((3,)), dma((3, 8)), dma((3,)), dma((3, 8)), dma((3,)), dma((3, 3)), dma((3,)), dma((3, 3)),
             ],
             compiler_params=pltpu.CompilerParams(collective_id=0, has_side_effects=True, vmem_limit_bytes=67043328),
             name='expert_layer',

time: 162 us -> 163 us (level)
  no operation moved by 1% of the time
where the time goes in v9:
time: 163 us; the launch traced here: 162 us
  Pallas kernels  161 us (99%)
  local copies, waits for them, and re-layouts  1.88 us (1%)
    pallas_call x1, Pallas kernels, device_fn(): pl.pallas_call(functools.partial(kernel, cols, cap, slots), out_shape=jax...  161 us

profile of v9, /device:TPU:1, one launch (start us, length us, event | category | flops | bytes accessed | tf_op | source)
XLA Modules:
  0.0 162.4 jit_solution(15692315712362081873)
XLA Ops:
  0.0 160.5 %expert_layer.1 = bf16[128,2048]{1,0:T(8,128)(2,1)} custom-call(bf16[128,2048]{1,0:T(8,128)(2,1)} %tokens_ref.1, s32[8,128]{1,0:T(8,128)} %bitcast.6, f32[8,128]{1,0:T(8,128)} %bitcast.7, bf16[2048,768]{1,0:T(8,128)(2,1)} %bitcast.4, bf16[768,2048]{1,0:T(8,128)(2,1)} %bitcast.5), custom_call_target="tpu_custom_call" | custom-call | tf_op jit(solution)/shard_map/expert_layer/pallas_call | solution.py:392
  160.5 1.9 %copy.7 = bf16[128,2048]{1,0:T(8,128)(2,1)} copy(bf16[128,2048]{1,0:T(8,128)(2,1)} %expert_layer.1) | data formatting | bytes 1048576

commit v10 on v9

--- a/solution.py
+++ b/solution.py
@@ -182,9 +182,6 @@
             for a in rest:
                 arrived(p, step, a)
             build(p, step)
-
-    load_in.wait()
-    load_out.wait()
 
     def halves(j):
         return (lax.div(j, 4), lax.rem(lax.div(j, 2), 2), lax.rem(j, 2))
@@ -310,12 +307,14 @@
             sums[p][s1 - 1] = mixed
             send(sums[p].at[s1 - 1], gots[p].at[s1 - 1], sum_send.at[p], sum_recv.at[p, s1 - 1], device(0, {AXES[p][0]: 4 - s1}))
 
-    pl.loop(0, 1)(expert)
-
     for p in range(3):
         for a in range(4):
             arrived(p, 2, a)
         build(p, 2)
+
+    load_in.wait()
+    load_out.wait()
+    pl.loop(0, 1)(expert)
 
     wait_for(cnt_in.at[pl.ds(1, 7)], cnt_recv)
     row = jnp.zeros((1, N), F32)

time: 163 us -> 163 us (level)
  no operation moved by 1% of the time
where the time goes in v10:
time: 163 us; the launch traced here: 162 us
  Pallas kernels  161 us (99%)
  local copies, waits for them, and re-layouts  1.88 us (1%)
    pallas_call x1, Pallas kernels, device_fn(): pl.pallas_call(functools.partial(kernel, cols, cap, slots), out_shape=jax...  161 us

profile of v10, /device:TPU:1, one launch (start us, length us, event | category | flops | bytes accessed | tf_op | source)
XLA Modules:
  0.0 162.4 jit_solution(15098955334468318780)
XLA Ops:
  0.0 160.5 %expert_layer.1 = bf16[128,2048]{1,0:T(8,128)(2,1)} custom-call(bf16[128,2048]{1,0:T(8,128)(2,1)} %tokens_ref.1, s32[8,128]{1,0:T(8,128)} %bitcast.6, f32[8,128]{1,0:T(8,128)} %bitcast.7, bf16[2048,768]{1,0:T(8,128)(2,1)} %bitcast.4, bf16[768,2048]{1,0:T(8,128)(2,1)} %bitcast.5), custom_call_target="tpu_custom_call" | custom-call | tf_op jit(solution)/shard_map/expert_layer/pallas_call | solution.py:391
  160.5 1.9 %copy.7 = bf16[128,2048]{1,0:T(8,128)(2,1)} copy(bf16[128,2048]{1,0:T(8,128)(2,1)} %expert_layer.1) | data formatting | bytes 1048576

commit v11 on v10

--- a/solution.py
+++ b/solution.py
@@ -301,11 +301,19 @@
         rows = ends[p][s1].reshape(32 * slots, cols[p][1])
         mixed = jnp.dot(scales[4 * p + s1], rows, preferred_element_type=F32)
         mixed = mixed[:tok] + (mixed[tok:2 * tok] + mixed[2 * tok:])
+        d1, low, high = AXES[p][0], pl.ds(0, half), pl.ds(half, half)
         if s1 == 0:
             acc[:, part(p)] = tokens_ref[:, part(p)].astype(F32) + mixed
-        else:
-            sums[p][s1 - 1] = mixed
-            send(sums[p].at[s1 - 1], gots[p].at[s1 - 1], sum_send.at[p], sum_recv.at[p, s1 - 1], device(0, {AXES[p][0]: 4 - s1}))
+            return
+        sums[p][s1 - 1] = mixed
+        if s1 == 2:
+            send(sums[p].at[1, low], gots[p].at[1, low], sum_send.at[p], sum_recv.at[p, 1], device(0, {d1: 3}))
+            send(sums[p].at[1, high], gots[p].at[1, high], sum_send.at[p], sum_recv.at[p, 3], device(0, {d1: 1}))
+            return
+        rows, sem = (low, 1) if s1 == 1 else (high, 3)
+        wait_for(gots[p].at[1, rows], sum_recv.at[p, sem])
+        sums[p][s1 - 1, rows] = sums[p][s1 - 1, rows] + gots[p][1, rows]
+        send(sums[p].at[s1 - 1], gots[p].at[s1 - 1], sum_send.at[p], sum_recv.at[p, s1 - 1], device(0, {d1: 4 - s1}))
 
     for p in range(3):
         for a in range(4):
@@ -348,6 +356,7 @@
     for p in range(3):
         wait_for(ends[p].at[pl.ds(2, 2), pl.ds(1, 3)], end_recv.at[p, 2])
         combine(p, 2)
+    for p in range(3):
         combine(p, 3)
     for p in range(3):
         wait_for(ends[p].at[pl.ds(1, 1), pl.ds(1, 3)], end_recv.at[p, 1])
@@ -358,7 +367,7 @@
 
     for p in range(3):
         total = acc[:, part(p)]
-        for i in range(3):
+        for i in (0, 2):
             wait_for(gots[p].at[i], sum_recv.at[p, i])
             total = total + gots[p][i]
         out_ref[:, part(p)] = total.astype(BF16)
@@ -412,7 +421,7 @@
                 pltpu.VMEM((1, N), F32),
                 pltpu.VMEM((tok, width), F32),
                 dma((2,)), dma((3,)), dma((3,)), dma((3, 16)), dma, dma, pltpu.SemaphoreType.REGULAR, dma((3,)), dma((3,)), dma((3, 16)),
-                dma((3,)), dma((3, 8)), dma((3,)), dma((3, 8)), dma((3,)), dma((3, 3)), dma((3,)), dma((3, 3)),
+                dma((3,)), dma((3, 8)), dma((3,)), dma((3, 8)), dma((3,)), dma((3, 3)), dma((3,)), dma((3, 4)),
             ],
             compiler_params=pltpu.CompilerParams(collective_id=0, has_side_effects=True, vmem_limit_bytes=67043328),
             name='expert_layer',

time: 163 us -> 163 us (level)
  no operation moved by 1% of the time
where the time goes in v11:
time: 163 us; the launch traced here: 162 us
  Pallas kernels  161 us (99%)
  local copies, waits for them, and re-layouts  1.88 us (1%)
    pallas_call x1, Pallas kernels, device_fn(): pl.pallas_call(functools.partial(kernel, cols, cap, slots), out_shape=jax...  161 us

profile of v11, /device:TPU:1, one launch (start us, length us, event | category | flops | bytes accessed | tf_op | source)
XLA Modules:
  0.0 162.4 jit_solution(16779948618480497556)
XLA Ops:
  0.0 160.5 %expert_layer.1 = bf16[128,2048]{1,0:T(8,128)(2,1)} custom-call(bf16[128,2048]{1,0:T(8,128)(2,1)} %tokens_ref.1, s32[8,128]{1,0:T(8,128)} %bitcast.6, f32[8,128]{1,0:T(8,128)} %bitcast.7, bf16[2048,768]{1,0:T(8,128)(2,1)} %bitcast.4, bf16[768,2048]{1,0:T(8,128)(2,1)} %bitcast.5), custom_call_target="tpu_custom_call" | custom-call | tf_op jit(solution)/shard_map/expert_layer/pallas_call | solution.py:400
  160.6 1.9 %copy.7 = bf16[128,2048]{1,0:T(8,128)(2,1)} copy(bf16[128,2048]{1,0:T(8,128)(2,1)} %expert_layer.1) | data formatting | bytes 1048576

commit v12 on v11

--- a/solution.py
+++ b/solution.py
@@ -347,15 +347,16 @@
     def _(i):
         pass_on(3 - i)
 
+    for p in range(3):
+        weigh(p)
+    for p in range(3):
+        wait_for(ends[p].at[pl.ds(2, 2), pl.ds(1, 3)], end_recv.at[p, 2])
+        combine(p, 2)
+
     for s2 in (1, 3, 2):
         for p in range(3):
             second(p, pl.ds(0, 1), s2, 0)
 
-    for p in range(3):
-        weigh(p)
-    for p in range(3):
-        wait_for(ends[p].at[pl.ds(2, 2), pl.ds(1, 3)], end_recv.at[p, 2])
-        combine(p, 2)
     for p in range(3):
         combine(p, 3)
     for p in range(3):

time: 163 us -> 159 us (0.975)
  Pallas kernels: 161 us -> 157 us
    pallas_call x1, Pallas kernels: 161 us -> 157 us  [device_fn(): pl.pallas_call(functools.partial(kernel, cols, cap, slots), out_shape=jax...]
where the time goes in v12:
time: 159 us
  Pallas kernels  157 us (99%)
  local copies, waits for them, and re-layouts  1.88 us (1%)
    pallas_call x1, Pallas kernels, device_fn(): pl.pallas_call(functools.partial(kernel, cols, cap, slots), out_shape=jax...  157 us

profile of v12, /device:TPU:1, one launch (start us, length us, event | category | flops | bytes accessed | tf_op | source)
XLA Modules:
  0.0 158.9 jit_solution(5830296189755665663)
XLA Ops:
  0.0 157.0 %expert_layer.1 = bf16[128,2048]{1,0:T(8,128)(2,1)} custom-call(bf16[128,2048]{1,0:T(8,128)(2,1)} %tokens_ref.1, s32[8,128]{1,0:T(8,128)} %bitcast.6, f32[8,128]{1,0:T(8,128)} %bitcast.7, bf16[2048,768]{1,0:T(8,128)(2,1)} %bitcast.4, bf16[768,2048]{1,0:T(8,128)(2,1)} %bitcast.5), custom_call_target="tpu_custom_call" | custom-call | tf_op jit(solution)/shard_map/expert_layer/pallas_call | solution.py:401
  157.0 1.9 %copy.7 = bf16[128,2048]{1,0:T(8,128)(2,1)} copy(bf16[128,2048]{1,0:T(8,128)(2,1)} %expert_layer.1) | data formatting | bytes 1048576

commit v13 on v12

--- a/solution.py
+++ b/solution.py
@@ -22,7 +22,7 @@
     return lax.broadcasted_iota(I32, shape, dim)
 
 
-def kernel(cols, cap, slots, tokens_ref, ids_ref, gates_ref, w_in_hbm, w_out_hbm, out_ref,
+def kernel(cols, back_cols, cap, slots, tokens_ref, ids_ref, gates_ref, w_in_hbm, w_out_hbm, out_ref,
            w_in, w_out, tok0, tok1, tok2, blk0, blk1, blk2, recv, mid0, mid1, mid2, end0, end1, end2,
            sum0, sum1, sum2, got0, got1, got2, info, info_all, places, scales, cnt_out, cnt_in, cnt_row, acc,
            w_sem, info_send_a, info_send_b, info_recv, cnt_send, cnt_recv, line_sem, tok_send_a, tok_send_b, tok_recv,
@@ -221,6 +221,12 @@
         o = recv[cube].reshape(rows, width)
         recv[cube] = jnp.where(keep, o, jnp.zeros_like(o)).reshape(2, 2, 2, 2, slots, width)
 
+    def back_part(p):
+        return pl.ds(back_cols[p][0], back_cols[p][1])
+
+    def wait_mid(p, blocks, sem):
+        wait_for(mids[p].at[0, pl.ds(0, 2), pl.ds(0, blocks // 2)], sem)
+
     def hand_out(j):
         high = halves(j)
         pair = [pl.ds(2 * h, 2) for h in high]
@@ -233,12 +239,12 @@
 
             @pl.when(high[d3] == 0)
             def _():
-                mids[p][(*rest, 0)] = recv[(0, *along(0), slice(None), part(p))]
+                mids[p][(*rest, 0)] = recv[(0, *along(0), slice(None), back_part(p))]
 
             @pl.loop(jnp.where(high[d3] == 0, 1, 0), 4)
             def _(i):
                 d_core, s3 = lax.div(i, 2), 2 * high[d3] + lax.rem(i, 2)
-                send(recv.at[(d_core, *along(s3), slice(None), part(p))], mids[p].at[(*rest, d_core * 4 + s3)],
+                send(recv.at[(d_core, *along(s3), slice(None), back_part(p))], mids[p].at[(*rest, d_core * 4 + s3)],
                      mid_send.at[p], mid_recv.at[p, j], device(d_core, {d3: 4 - s3}))
 
     def middle(p, s1, s2):
@@ -255,8 +261,8 @@
 
             @pl.when(high[d3] == 0)
             def _():
-                wait_blocks(p, 1, blks[p], mid_recv.at[p, j + (4, 2, 1)[d3]])
-                wait_blocks(p, 0, blks[p], mid_recv.at[p, j])
+                wait_mid(p, 16, mid_recv.at[p, j + (4, 2, 1)[d3]])
+                wait_mid(p, 12, mid_recv.at[p, j])
                 first = pl.ds(2 * high[d1], 2)
 
                 @pl.when(high[d2] == 0)
@@ -298,12 +304,12 @@
             scales[4 * p + s1] = jnp.concatenate([high, mid, low], axis=0)
 
     def combine(p, s1):
-        rows = ends[p][s1].reshape(32 * slots, cols[p][1])
+        rows = ends[p][s1].reshape(32 * slots, back_cols[p][1])
         mixed = jnp.dot(scales[4 * p + s1], rows, preferred_element_type=F32)
         mixed = mixed[:tok] + (mixed[tok:2 * tok] + mixed[2 * tok:])
         d1, low, high = AXES[p][0], pl.ds(0, half), pl.ds(half, half)
         if s1 == 0:
-            acc[:, part(p)] = tokens_ref[:, part(p)].astype(F32) + mixed
+            acc[:, back_part(p)] = tokens_ref[:, back_part(p)].astype(F32) + mixed
             return
         sums[p][s1 - 1] = mixed
         if s1 == 2:
@@ -367,11 +373,11 @@
         combine(p, 0)
 
     for p in range(3):
-        total = acc[:, part(p)]
+        total = acc[:, back_part(p)]
         for i in (0, 2):
             wait_for(gots[p].at[i], sum_recv.at[p, i])
             total = total + gots[p][i]
-        out_ref[:, part(p)] = total.astype(BF16)
+        out_ref[:, back_part(p)] = total.astype(BF16)
 
     wait_for(cnt_in.at[pl.ds(1, 7)], cnt_send)
     for p in range(3):
@@ -395,11 +401,13 @@
         tiles = width // 128
         sizes = [128 * (tiles // 3 + (1 if p < tiles % 3 else 0)) for p in range(3)]
         cols = [(sum(sizes[:p]), sizes[p]) for p in range(3)]
+        back = sizes[::-1]
+        back_cols = [(sum(back[:p]), back[p]) for p in range(3)]
         vmem = pl.BlockSpec(memory_space=pltpu.VMEM)
         anyspace = pl.BlockSpec(memory_space=pl.ANY)
         dma = pltpu.SemaphoreType.DMA
         return pl.pallas_call(
-            functools.partial(kernel, cols, cap, slots),
+            functools.partial(kernel, cols, back_cols, cap, slots),
             out_shape=jax.ShapeDtypeStruct((tok, width), BF16),
             in_specs=[vmem, vmem, vmem, anyspace, anyspace],
             out_specs=vmem,
@@ -409,10 +417,10 @@
                 *[pltpu.VMEM((4, 4, tok, s), BF16) for s in sizes],
                 *[pltpu.VMEM((4, 8, 4, slots, s), BF16) for s in sizes],
                 pltpu.VMEM((2, 4, 4, 4, slots, width), BF16),
-                *[pltpu.VMEM((4, 4, 8, slots, s), BF16) for s in sizes],
-                *[pltpu.VMEM((4, 4, 8, slots, s), BF16) for s in sizes],
-                *[pltpu.VMEM((3, tok, s), F32) for s in sizes],
-                *[pltpu.VMEM((3, tok, s), F32) for s in sizes],
+                *[pltpu.VMEM((4, 4, 8, slots, s), BF16) for s in back],
+                *[pltpu.VMEM((4, 4, 8, slots, s), BF16) for s in back],
+                *[pltpu.VMEM((3, tok, s), F32) for s in back],
+                *[pltpu.VMEM((3, tok, s), F32) for s in back],
                 pltpu.VMEM((2 * top, tok), F32),
                 pltpu.VMEM((3, 16, 2 * top, tok), F32),
                 pltpu.VMEM((32, tok), F32),

time: 159 us -> 160 us (level); the launches traced: 159 us -> 158 us
  no operation moved by 1% of the time
where the time goes in v13:
time: 160 us; the launch traced here: 158 us
  Pallas kernels  156 us (98%)
  local copies, waits for them, and re-layouts  1.88 us (1%)
    pallas_call x1, Pallas kernels, device_fn(): pl.pallas_call(functools.partial(kernel, cols, back_cols, cap, slots), ou...  156 us

profile of v13, /device:TPU:1, one launch (start us, length us, event | category | flops | bytes accessed | tf_op | source)
XLA Modules:
  0.0 158.1 jit_solution(13473115725436667909)
XLA Ops:
  0.0 156.2 %expert_layer.1 = bf16[128,2048]{1,0:T(8,128)(2,1)} custom-call(bf16[128,2048]{1,0:T(8,128)(2,1)} %tokens_ref.1, s32[8,128]{1,0:T(8,128)} %bitcast.6, f32[8,128]{1,0:T(8,128)} %bitcast.7, bf16[2048,768]{1,0:T(8,128)(2,1)} %bitcast.4, bf16[768,2048]{1,0:T(8,128)(2,1)} %bitcast.5), custom_call_target="tpu_custom_call" | custom-call | tf_op jit(solution)/shard_map/expert_layer/pallas_call | solution.py:409
  156.2 1.9 %copy.7 = bf16[128,2048]{1,0:T(8,128)(2,1)} copy(bf16[128,2048]{1,0:T(8,128)(2,1)} %expert_layer.1) | data formatting | bytes 1048576
